TPU v7x, 512 devices: a whole 4x8x8 slice. The times are simulated.
512 devices in a mesh: step: 16 (over y_lo, x), seq: 32 (over z, y_hi, core).
Axes of the slice: x: 4, y: 8 (y_hi: 2, y_lo: 4; y = y_hi * 4 + y_lo), z: 8, core: 2. Of those that a mesh axis runs over, the one named last changes fastest.
Arguments:
- latents: float32 [16, 1024, 64], P('step', 'seq'), may hold values from -6 to 6
- timesteps: int32 [17], replicated, may hold values from 0 to 1000, as said below
- embed_weight: bfloat16 [64, 4096], replicated, may hold values from -0.75 to 0.75
- mod_weight: float32 [256, 2, 4096], P('seq'), may hold values from -0.375 to 0.375
- qkv_weight: bfloat16 [4096, 32, 3, 128], P('step', 'seq'), may hold values from -0.09375 to 0.09375
- out_weight: bfloat16 [32, 128, 64], P('seq'), may hold values from -6 to 6
Outputs:
- updated: float32 [16, 1024, 64], P('step', 'seq')
- velocity: float32 [16, 1024, 64], P('step', 'seq')
Inputs may be any that keep to these rules, and one draw needn't show every extreme that they name: `timesteps`: strictly decreasing along the table.
All inputs are finite; a program needn't handle non-finite values.
Results may differ from a plain program's by a relative error of at most 0.0049.
Values may be sent and summed in bfloat16 or wider, within the bound.
No kernel may reach another device: no remote copies, remote signals or barrier semaphores. Data moves between devices by JAX's collectives and lax.ppermute only.
A program may use at most 64 MiB of HBM per device.

v0:
```python
import math

import jax
import jax.numpy as jnp
from jax import lax
from jax.sharding import Mesh
from jax.sharding import PartitionSpec as P

FREQ = 256
STEP = ("step_0", "step_1")


def sent_to_all(shard, axis):
    copies = jnp.broadcast_to(shard, (lax.axis_size(axis), *shard.shape))
    return lax.all_to_all(copies, axis, split_axis=0, concat_axis=0, tiled=True)


def over_copies(shard, axis):
    return sent_to_all(shard, axis).sum(axis=0)


def in_order(pieces, dim):
    pieces = jnp.moveaxis(pieces, 0, dim)
    shape = pieces.shape
    return pieces.reshape(*shape[:dim], shape[dim] * shape[dim + 1], *shape[dim + 2 :])


def gather_directly(shard, axis, dim):
    return in_order(sent_to_all(shard, axis), dim)


def gather_in_order(shard, axes, order):
    pieces = shard
    for k in order:
        pieces = lax.all_gather(pieces, axes[k])
    done = order[::-1]
    back = [done.index(k) for k in range(len(axes))]
    pieces = pieces.transpose(*back, *range(len(axes), pieces.ndim))
    return pieces.reshape(-1, *shard.shape)


def gather_axes(shard, axes, order, dim):
    return in_order(gather_in_order(shard, axes, order), dim)


def in_blocks(shard, dim, devices):
    before, after = (shard.shape[:dim], shard.shape[dim + 1 :])
    return jnp.moveaxis(shard.reshape(*before, devices, -1, *after), dim, 0)


def summed_on_arrival(shard, axis, dim):
    pieces = in_blocks(shard, dim, lax.axis_size(axis))
    arrived = lax.all_to_all(pieces, axis, split_axis=0, concat_axis=0, tiled=True)
    return arrived.astype(jnp.float32).sum(axis=0)


def condition_of(stamp):
    half_count = FREQ // 2
    frequencies = jnp.exp(
        -math.log(10000.0) * jnp.arange(half_count, dtype=jnp.float32) / half_count
    )
    angles = stamp * frequencies
    return jnp.concatenate([jnp.cos(angles), jnp.sin(angles)])


def modulate(latent_rows, embed_weight, shift_vec, scale_vec):
    embedded = jnp.dot(latent_rows, embed_weight, preferred_element_type=jnp.float32)
    center_mean = jnp.mean(embedded, axis=-1, keepdims=True)
    centered = embedded - center_mean
    variance = jnp.mean(centered * centered, axis=-1, keepdims=True)
    normed = centered * lax.rsqrt(variance + 1e-06)
    return (normed * (1.0 + scale_vec) + shift_vec).astype(jnp.bfloat16)


def qk_norm(head_rows):
    as_float = head_rows.astype(jnp.float32)
    return (
        as_float * lax.rsqrt(jnp.mean(as_float * as_float, axis=-1, keepdims=True) + 1e-06)
    ).astype(jnp.bfloat16)


def attend_head(head_block):
    queries = qk_norm(head_block[:, 0])
    key_rows = qk_norm(head_block[:, 1])
    values = head_block[:, 2]
    seq_length = queries.shape[0]
    head_dim = queries.shape[1]
    block_rows = math.gcd(seq_length, 512)
    query_blocks = queries.reshape(seq_length // block_rows, block_rows, head_dim)

    def one_block(query_block):
        scores = jnp.dot(query_block, key_rows.T, preferred_element_type=jnp.float32) * (
            1.0 / math.sqrt(head_dim)
        )
        weights = jnp.exp(scores)
        probabilities = (weights / jnp.sum(weights, axis=-1, keepdims=True)).astype(jnp.bfloat16)
        return jnp.dot(probabilities, values, preferred_element_type=jnp.float32).astype(
            jnp.bfloat16
        )

    return lax.map(one_block, query_blocks).reshape(seq_length, head_dim)


def on_device(latents, timesteps, embed_weight, mod_weight, qkv_weight, out_weight):
    step_index = lax.axis_index(STEP)
    seq_index = lax.axis_index("seq")
    stamp_pair = lax.dynamic_slice_in_dim(timesteps, step_index, 2, 0).astype(jnp.float32)
    condition_vec = condition_of(stamp_pair[0])
    feature_rows = mod_weight.shape[0]
    local_features = lax.dynamic_slice_in_dim(
        condition_vec, seq_index * feature_rows, feature_rows, 0
    )
    partial_mod = jnp.einsum(
        "f,fcd->cd", local_features, mod_weight, precision=lax.Precision.HIGHEST
    )
    modulation = over_copies(partial_mod, "seq")
    own_latents = latents[0].astype(jnp.bfloat16)
    all_latents = gather_directly(own_latents, "seq", 0)
    gathered = modulate(all_latents, embed_weight, modulation[0], modulation[1])
    seq_length = gathered.shape[0]
    heads_here = qkv_weight.shape[1]
    head_dim = qkv_weight.shape[3]
    qkv_width = heads_here * 3 * head_dim
    weight_piece = gather_axes(qkv_weight, STEP, (0, 1), 0)
    flat_piece = weight_piece.reshape(weight_piece.shape[0], qkv_width)
    accumulated = jnp.dot(gathered, flat_piece, preferred_element_type=jnp.float32)
    projected = accumulated.astype(jnp.bfloat16).reshape(seq_length, heads_here, 3, head_dim)
    attended = lax.map(attend_head, jnp.moveaxis(projected, 1, 0))
    merged_heads = jnp.moveaxis(attended, 0, 1).reshape(seq_length, heads_here * head_dim)
    out_matrix = out_weight.reshape(heads_here * head_dim, out_weight.shape[2])
    velocity = summed_on_arrival(
        jnp.dot(merged_heads, out_matrix, preferred_element_type=jnp.float32).astype(jnp.bfloat16),
        "seq",
        0,
    )
    step_size = (stamp_pair[1] - stamp_pair[0]) / 1000.0
    increment = step_size * velocity + jnp.where(
        step_index == 0, latents[0], jnp.zeros_like(latents[0])
    )
    every_term = gather_directly(increment[None], STEP, 0)
    lower_mask = jnp.arange(every_term.shape[0], dtype=jnp.int32) < step_index
    earlier = jnp.sum(jnp.where(lower_mask[:, None, None], every_term, 0.0), axis=0)
    updated = earlier + increment
    return (updated[None], velocity[None])


def solution(mesh):
    split = Mesh(mesh.devices.reshape(4, 4, mesh.shape["seq"]), ("step_0", "step_1", "seq"))
    return jax.shard_map(
        on_device,
        mesh=split,
        in_specs=(
            P(STEP, "seq", None),
            P(),
            P(),
            P("seq", None, None),
            P(STEP, "seq", None, None),
            P("seq", None, None),
        ),
        out_specs=(P(STEP, "seq", None), P(STEP, "seq", None)),
        check_vma=False,
    )
```

profile of v0, /device:TPU:1, one launch (start us, length us, event | category | flops | bytes accessed | tf_op | source)
XLA Modules:
  0.0 169.6 jit_solution(11054272650411639578)
XLA Ops:
  7.2 17.8 %all-gather = bf16[1024,1,3,128]{3,0,2,1:T(8,128)(2,1)} all-gather(bf16[256,1,3,128]{3,0,2,1:T(8,128)(2,1)} %param.12), channel_id=2, replica_groups=mesh['step_0'=4,'step_1'=4,'seq'=32] {'step_0'}, dimensions={0}, use_global_device_ids=true | all-gather | bytes 983040 | tf_op jit(solution)/shard_map/all_gather | solution.py:35
  25.1 0.7 convert_bitcast_fusion
  25.8 0.8 reshape.96
  26.7 18.3 %all-to-all-start = ((bf16[32,2,1024]{2,1,0:T(2,128)(2,1)}), bf16[32,2,1024]{2,1,0:T(2,128)(2,1)S(1)}, u32[]{:S(2)}, u32[]{:S(2)}) async-start(bf16[32,2,1024]{2,1,0:T(2,128)(2,1)} %reshape.96), calls=%async_computation | async-start | bytes 262144 | tf_op jit(solution)/shard_map/all_to_all | solution.py:15
  45.0 0.7 dynamic-slice_convert_fusion
  47.1 1.5 fusion.13
  48.6 8.8 %all-to-all-done = bf16[32,2,1024]{2,1,0:T(2,128)(2,1)S(1)} async-done(((bf16[32,2,1024]{2,1,0:T(2,128)(2,1)}), bf16[32,2,1024]{2,1,0:T(2,128)(2,1)S(1)}, u32[]{:S(2)}, u32[]{:S(2)}) %all-to-all-start) | async-done | bytes 131104 | tf_op jit(solution)/shard_map/all_to_all | solution.py:15
  57.4 1.5 broadcast_in_dim.46
  58.8 4.3 %all-to-all-start.1 = ((f32[32,2,4096]{2,1,0:T(2,128)}), f32[32,2,4096]{2,1,0:T(2,128)S(1)}, u32[]{:S(2)}, u32[]{:S(2)}) async-start(f32[32,2,4096]{2,1,0:T(2,128)} %broadcast_in_dim.46), calls=%async_computation.1 | async-start | bytes 2097152 | tf_op jit(solution)/shard_map/all_to_all | solution.py:15
  63.4 8.0 %fusion.22 = (f32[1024]{0:T(1024)S(1)}, f32[1024,4096]{1,0:T(8,128)}) fusion(bf16[1024,64]{1,0:T(8,128)(2,1)S(1)} %bitcast.69, bf16[64,4096]{1,0:T(8,128)(2,1)S(1)} %copy-done), kind=kOutput, calls=%fused_computation.48 | convolution fusion | flops 541064192 | bytes 17436672 | tf_op jit(solution)/shard_map/dot_general | solution.py:67
  71.4 7.5 %multiply_reduce_fusion = f32[1024]{0:T(1024)S(1)} fusion(f32[1024,4096]{1,0:T(8,128)} %get-tuple-element.59, f32[1024]{0:T(1024)S(1)} %broadcast_multiply_fusion), kind=kLoop, calls=%fused_computation.12 | loop fusion | flops 12581888 | bytes 16785408 | tf_op jit(solution)/shard_map/reduce_sum | solution.py:70
  79.0 14.5 %all-to-all-done.1 = f32[32,2,4096]{2,1,0:T(2,128)S(1)} async-done(((f32[32,2,4096]{2,1,0:T(2,128)}), f32[32,2,4096]{2,1,0:T(2,128)S(1)}, u32[]{:S(2)}, u32[]{:S(2)}) %all-to-all-start.1) | async-done | bytes 1048608 | tf_op jit(solution)/shard_map/all_to_all | solution.py:15
  93.9 3.9 %copy.39 = bf16[16,256,1,3,128]{4,1,3,2,0:T(8,128)(2,1)} copy(bf16[16,256,1,3,128]{4,1,0,3,2:T(8,128)(2,1)} %all-gather.4.cloned.1.call-done) | data formatting | bytes 6291456 | tf_op jit(solution)/shard_map/all_gather | solution.py:35
  97.8 6.3 %copy.40 = bf16[4,4,256,1,3,128]{2,1,0,5,4,3:T(4,128)(2,1)} copy(bf16[4,4,256,1,3,128]{5,2,4,3,0,1:T(8,128)(2,1)} %bitcast.64) | data formatting | bytes 6291456 | tf_op jit(solution)/shard_map/transpose | solution.py:38
  104.1 6.1 %reshape_reshape_reshape.3 = bf16[4096,384]{0,1:T(8,128)(2,1)} reshape(bf16[4,4,256,1,3,128]{2,1,0,5,4,3:T(4,128)(2,1)} %copy.40) | data formatting | bytes 6291456 | tf_op jit(solution)/shard_map/reshape;reshape;reshape | solution.py:125
  110.2 10.3 %fusion.9 = bf16[1024,384]{0,1:T(8,128)(2,1)S(1)} fusion(bf16[4096,384]{0,1:T(8,128)(2,1)} %reshape_reshape_reshape.3, f32[1024,4096]{1,0:T(8,128)} %get-tuple-element.59, f32[4096]{0:T(1024)S(1)} %bitcast.76, f32[4096]{0:T(1024)S(1)} %bitcast.75, f32[1024]{0:T(1024)S(1)} %add_rsqrt_fusion.2, f32[1024]{0:T(1024)S(1)} %broadcast_multiply_fusion), kind=kOutput, calls=%fused_computation.14 | convolution fusion | flops 3242590208 | bytes 20750336 | tf_op jit(solution)/shard_map/dot_general | solution.py:126
  121.9 2.3 %while.17 = (s32[]{:T(128)}, bf16[2,512,128]{2,1,0:T(8,128)(2,1)S(1)}, bf16[2,512,128]{2,1,0:T(8,128)(2,1)S(1)}, bf16[1024,128]{1,0:T(8,128)(2,1)S(1)}, bf16[1024,128]{1,0:T(8,128)(2,1)S(1)}, /*index=5*/s32[]{:T(128)}) while((s32[]{:T(128)}, bf16[2,512,128]{2,1,0:T(8,128)(2,1)S(1)}, bf16[2,512,128]{2,1,0:T(8,128)(2,1)S(1)}, ...), condition=%wide.region_7.0_spmd, body=%wide.region_5.7_spmd.sunk | while | flops 271121920 | bytes 4984917 | solution.py:101
  124.6 0.8 reshape.98
  125.4 6.5 %all-to-all-start.2 = ((bf16[32,2,1024]{2,1,0:T(2,128)(2,1)}), bf16[32,2,1024]{2,1,0:T(2,128)(2,1)S(1)}, u32[]{:S(2)}, u32[]{:S(2)}) async-start(bf16[32,2,1024]{2,1,0:T(2,128)(2,1)} %reshape.98), calls=%async_computation.2 | async-start | bytes 262144 | tf_op jit(solution)/shard_map/all_to_all | solution.py:53
  133.2 11.2 %all-to-all-done.2 = bf16[32,2,1024]{2,1,0:T(2,128)(2,1)S(1)} async-done(((bf16[32,2,1024]{2,1,0:T(2,128)(2,1)}), bf16[32,2,1024]{2,1,0:T(2,128)(2,1)S(1)}, u32[]{:S(2)}, u32[]{:S(2)}) %all-to-all-start.2) | async-done | bytes 131104 | tf_op jit(solution)/shard_map/all_to_all | solution.py:53
  144.7 0.8 reshape.100
  145.5 7.1 %all-to-all-start.3 = ((f32[16,1,2048]{2,1,0:T(1,128)}), f32[16,1,2048]{2,1,0:T(1,128)S(1)}, u32[]{:S(2)}, u32[]{:S(2)}) async-start(f32[16,1,2048]{2,1,0:T(1,128)} %reshape.100), calls=%async_computation.3 | async-start | bytes 262144 | tf_op jit(solution)/shard_map/all_to_all | solution.py:15
  152.6 7.8 %all-to-all-done.3 = f32[16,1,2048]{2,1,0:T(1,128)S(1)} async-done(((f32[16,1,2048]{2,1,0:T(1,128)}), f32[16,1,2048]{2,1,0:T(1,128)S(1)}, u32[]{:S(2)}, u32[]{:S(2)}) %all-to-all-start.3) | async-done | bytes 131104 | tf_op jit(solution)/shard_map/all_to_all | solution.py:15
  161.0 0.9 reduce.1
  (48 shorter events, 7.6 us)
Async XLA Ops:
  7.2 56.2 %copy-start = (bf16[64,4096]{1,0:T(8,128)(2,1)S(1)}, bf16[64,4096]{1,0:T(8,128)(2,1)}, u32[]{:S(2)}) copy-start(bf16[64,4096]{1,0:T(8,128)(2,1)} %param.10) | copy-start | bytes 1572868
  7.2 86.7 %all-gather.4.cloned.1.call-start = ((), (), s32[]{:S(2)}) async-start(), calls=%async_computation.4 | async-start | bytes 3932160 | tf_op jit(solution)/shard_map/all_gather | solution.py:35
  26.7 30.7 %all-to-all-start = ((bf16[32,2,1024]{2,1,0:T(2,128)(2,1)}), bf16[32,2,1024]{2,1,0:T(2,128)(2,1)S(1)}, u32[]{:S(2)}, u32[]{:S(2)}) async-start(bf16[32,2,1024]{2,1,0:T(2,128)(2,1)} %reshape.96), calls=%async_computation | async-start | bytes 262144 | tf_op jit(solution)/shard_map/all_to_all | solution.py:15
  58.8 34.7 %all-to-all-start.1 = ((f32[32,2,4096]{2,1,0:T(2,128)}), f32[32,2,4096]{2,1,0:T(2,128)S(1)}, u32[]{:S(2)}, u32[]{:S(2)}) async-start(f32[32,2,4096]{2,1,0:T(2,128)} %broadcast_in_dim.46), calls=%async_computation.1 | async-start | bytes 2097152 | tf_op jit(solution)/shard_map/all_to_all | solution.py:15
  121.9 2.3 %copy-start.3 = (bf16[1,128,64]{1,2,0:T(8,128)(2,1)S(1)}, bf16[1,128,64]{1,2,0:T(8,128)(2,1)}, u32[]{:S(2)}) copy-start(bf16[1,128,64]{1,2,0:T(8,128)(2,1)} %param.13) | copy-start | bytes 49156
  121.9 22.7 %copy-start.2 = (f32[1,32,64]{2,1,0:T(8,128)S(1)}, f32[1,32,64]{2,1,0:T(8,128)}, u32[]{:S(2)}) copy-start(f32[1,32,64]{2,1,0:T(8,128)} %param.8) | copy-start | bytes 24580
  125.4 18.9 %all-to-all-start.2 = ((bf16[32,2,1024]{2,1,0:T(2,128)(2,1)}), bf16[32,2,1024]{2,1,0:T(2,128)(2,1)S(1)}, u32[]{:S(2)}, u32[]{:S(2)}) async-start(bf16[32,2,1024]{2,1,0:T(2,128)(2,1)} %reshape.98), calls=%async_computation.2 | async-start | bytes 262144 | tf_op jit(solution)/shard_map/all_to_all | solution.py:53
  144.6 18.1 %copy-start.1 = (f32[32,64]{1,0:T(8,128)}, f32[32,64]{1,0:T(8,128)S(1)}, u32[]{:S(2)}) copy-start(f32[32,64]{1,0:T(8,128)S(1)} %convert_reduce_fusion) | copy-start | bytes 24580
  145.5 15.0 %all-to-all-start.3 = ((f32[16,1,2048]{2,1,0:T(1,128)}), f32[16,1,2048]{2,1,0:T(1,128)S(1)}, u32[]{:S(2)}, u32[]{:S(2)}) async-start(f32[16,1,2048]{2,1,0:T(1,128)} %reshape.100), calls=%async_computation.3 | async-start | bytes 262144 | tf_op jit(solution)/shard_map/all_to_all | solution.py:15
Sparse Core Ops, SparseCore 0:
  25.2 51.2 all-gather.3
where the time goes:
time: 170 us
  waiting for transfers between devices  42.4 us (25%)
  starting transfers between devices  36.2 us (21%)
  local copies, waits for them, and re-layouts  22.7 us (13%)
  matrix products  22.2 us (13%)
  blocking collectives  17.8 us (10%)
  between operations  15.6 us (9%)
  other arithmetic  12.6 us (7%)
    all_to_all x3, waiting for transfers between devices, sent_to_all(): return lax.all_to_all(copies, axis, split_axis=0, concat_axis=0, tiled=True)  31.2 us
    all_to_all x3, starting transfers between devices, sent_to_all(): return lax.all_to_all(copies, axis, split_axis=0, concat_axis=0, tiled=True)  29.7 us
    all_gather x1, blocking collectives, gather_in_order(): pieces = lax.all_gather(pieces, axes[k])  17.8 us
    all_to_all x1, waiting for transfers between devices, summed_on_arrival(): lax.all_to_all(pieces, axis, split_axis=0, concat_axis=0, tiled=True)  11.2 us
    dot_general x1, matrix products, on_device(): jnp.dot(gathered, flat_piece, preferred_element_type=jnp.float32)  10.3 us
    dot_general x1, matrix products, modulate(): jnp.dot(latent_rows, embed_weight, preferred_element_type=jnp.float32)  8.04 us
    reduce_sum x1, other arithmetic, modulate(): variance = jnp.mean(centered * centered, axis=-1, keepdims=True)  7.54 us
    all_to_all x1, starting transfers between devices, summed_on_arrival(): lax.all_to_all(pieces, axis, split_axis=0, concat_axis=0, tiled=True)  6.46 us
  transfers between devices with their start and end apart: 5, of which 4 were waited for; matrix products, arithmetic and copies ran while one was open for 13% of the time, Pallas kernels for 0%

commit v1 on v0

v1 whole, which is shorter than its diff:
```python
import math

import jax
import jax.numpy as jnp
from jax import lax
from jax.experimental import pallas as pl
from jax.experimental.pallas import tpu as pltpu
from jax.sharding import Mesh
from jax.sharding import PartitionSpec as P

STEP = ("y_lo", "x")
SEQ = ("z", "y_hi", "core")
BF = jnp.bfloat16
F32 = jnp.float32
LN = 128
SMEM = pltpu.SMEM


def dot(a, b):
    return jnp.dot(a, b, preferred_element_type=F32)


def dot_t(a, b):
    return lax.dot_general(a, b, (((1,), (1,)), ((), ())), preferred_element_type=F32)


def halves(x):
    hi = x.astype(BF)
    return hi, (x - hi.astype(F32)).astype(BF)


def low_lanes(shape):
    return lax.broadcasted_iota(jnp.int32, shape, len(shape) - 1) < LN // 2


def pack_rows(rows):
    return jnp.concatenate([rows[:16], rows[16:]], axis=1)


def pack_kernel(at_ref, lat_ref, mw_ref, out_ref):
    lat = pack_rows(lat_ref[0]).astype(BF)
    by_kind = [mw_ref[:, 0, :], mw_ref[:, 1, :]]
    blocks = [lat]
    lows = []
    for part in range(2):
        cols = slice(part * LN, (part + 1) * LN)
        hi, lo = halves(jnp.concatenate([by_kind[0][:, cols], by_kind[1][:, cols]], axis=0))
        blocks.append(hi)
        lows.append(lo)
    payload = jnp.concatenate(blocks + lows, axis=0)
    for peer in range(out_ref.shape[0]):
        out_ref[peer] = payload


def pack(at, latents, mod_weight, peers):
    width = mod_weight.shape[2] // 16
    return pl.pallas_call(
        pack_kernel,
        grid_spec=pltpu.PrefetchScalarGridSpec(
            num_scalar_prefetch=1,
            grid=(1,),
            in_specs=[
                pl.BlockSpec(latents.shape, lambda i, at: (0, 0, 0)),
                pl.BlockSpec((8, 2, width), lambda i, at: (0, 0, at[0])),
            ],
            out_specs=pl.BlockSpec((peers, 80, LN), lambda i, at: (0, 0, 0)),
        ),
        out_shape=jax.ShapeDtypeStruct((peers, 80, LN), BF),
        name="pack",
    )(at, latents, mod_weight)


def weights_kernel(at_ref, embed_ref, part_ref, w_ref, out_ref, centered_ref, gram_ref, wv_ref):
    embed = embed_ref[...].astype(F32)
    mean = jnp.mean(embed, axis=1, keepdims=True)
    centered_ref[...] = part_ref[...].astype(F32) - mean
    hi, lo = halves(embed - mean)
    hi2 = jnp.concatenate([hi, hi], axis=0)
    lo2 = jnp.concatenate([lo, lo], axis=0)
    gram = (dot_t(hi2, hi2) + dot_t(hi2, lo2) + dot_t(lo2, hi2)) * (1.0 / embed.shape[1])
    row = lax.broadcasted_iota(jnp.int32, gram.shape, 0) < LN // 2
    gram = jnp.where(row == low_lanes(gram.shape), gram, 0.0)
    gram_ref[0], gram_ref[1] = halves(gram)
    out = out_ref[0]
    wv_ref[0], wv_ref[1] = halves(dot(w_ref[...], jnp.concatenate([out, out], axis=1)))


def weights(at, embed_weight, wv, out_weight):
    width = wv.shape[0]
    channels = embed_weight.shape[0]
    return pl.pallas_call(
        weights_kernel,
        grid_spec=pltpu.PrefetchScalarGridSpec(
            num_scalar_prefetch=1,
            grid=(1,),
            in_specs=[
                pl.BlockSpec(embed_weight.shape, lambda i, at: (0, 0)),
                pl.BlockSpec((channels, width), lambda i, at: (0, at[0])),
                pl.BlockSpec(wv.shape, lambda i, at: (0, 0)),
                pl.BlockSpec(out_weight.shape, lambda i, at: (0, 0, 0)),
            ],
            out_specs=[
                pl.BlockSpec((channels, width), lambda i, at: (0, 0)),
                pl.BlockSpec((2, LN, LN), lambda i, at: (0, 0, 0)),
                pl.BlockSpec((2, width, LN), lambda i, at: (0, 0, 0)),
            ],
        ),
        out_shape=[
            jax.ShapeDtypeStruct((channels, width), F32),
            jax.ShapeDtypeStruct((2, LN, LN), BF),
            jax.ShapeDtypeStruct((2, width, LN), BF),
        ],
        name="weights",
    )(at, embed_weight, embed_weight, wv, out_weight)


def partial_kernel(mod_ref, cond_ref, centered_ref, w_ref, wv_ref, out_ref):
    cond = cond_ref[...]
    cond_hi, cond_lo = halves(cond)
    cond2 = jnp.concatenate([cond_hi, cond_lo], axis=0)
    parts = []
    for part in range(2):
        hi = mod_ref[:, :, 16 + part * 16 : 32 + part * 16, :].reshape(512, LN)
        lo = mod_ref[:, :, 48 + part * 16 : 64 + part * 16, :].reshape(512, LN)
        both = dot(cond2, hi)
        parts.append(both[:32] + both[32:] + dot(cond_hi, lo))
    modulation = jnp.concatenate(parts, axis=1)
    shift, scale = modulation[:16], modulation[16:] + 1.0
    centered = centered_ref[...]
    rows = jnp.concatenate(
        [(centered * scale[k : k + 1]).astype(BF) for k in range(16)], axis=0
    )
    shift2 = jnp.concatenate(halves(shift), axis=0)
    wq, wk, wv_hi, wv_lo = w_ref[0], w_ref[1], wv_ref[0], wv_ref[1]
    mq = dot(rows, wq)
    mk = dot(rows, wk)
    mv = dot(rows, wv_hi) + dot(rows, wv_lo)
    biases = []
    for w in (wq, wk, wv_hi):
        b = dot(shift2, w)
        biases.append(b[:16] + b[16:])
    biases[2] = biases[2] + dot(shift2[:16], wv_lo)
    line = lax.broadcasted_iota(jnp.int32, (16, LN), 0)
    low = low_lanes((32, LN))
    for k in range(16):
        at = slice(k * 64, k * 64 + 64)
        out_ref[k, 0:64] = mq[at].astype(BF)
        out_ref[k, 64:128] = mk[at].astype(BF)
        v = mv[at]
        out_ref[k, 128:160] = jnp.where(low, v[:32], v[32:]).astype(BF)
        tile = jnp.where(line == 0, biases[0][k : k + 1], 0.0)
        tile = jnp.where(line == 1, biases[1][k : k + 1], tile)
        tile = jnp.where(line == 2, biases[2][k : k + 1], tile)
        out_ref[k, 160:176] = tile.astype(BF)


def attend_kernel(parts_ref, lat_ref, gram_ref, out_ref):
    total = jnp.sum(parts_ref[...].astype(F32), axis=0)
    mq, mk, mv = total[0:64], total[64:128], total[128:160]
    low32 = low_lanes((32, LN))
    turned = pltpu.roll(mv, LN // 2, 1)
    mv = jnp.concatenate(
        [jnp.where(low32, mv, turned), jnp.where(low32, turned, mv)], axis=0
    )
    bias_q, bias_k, bias_v = total[160:161], total[161:162], total[162:163]
    packed = lat_ref[...].reshape(512, LN)
    as_float = packed.astype(F32)
    square = (dot(packed, gram_ref[0]) + dot(packed, gram_ref[1])) * as_float
    low = low_lanes((512, LN))
    gain_low = lax.rsqrt(jnp.sum(jnp.where(low, square, 0.0), axis=1, keepdims=True) + 1e-06)
    gain_high = lax.rsqrt(jnp.sum(jnp.where(low, 0.0, square), axis=1, keepdims=True) + 1e-06)
    twice = jnp.concatenate([packed, packed], axis=1)
    none = jnp.zeros((64, LN), BF)

    def project(m, bias):
        hi, lo = halves(m)
        first = dot(twice, jnp.concatenate([hi, none, lo, none], axis=0))
        second = dot(twice, jnp.concatenate([none, hi, none, lo], axis=0))
        return gain_low * first + bias, gain_high * second + bias

    def unit(u, factor):
        mean = jnp.mean(u * u, axis=1, keepdims=True)
        return (u * (lax.rsqrt(mean + 1e-06) * factor)).astype(BF)

    q_low, q_high = (unit(u, math.log2(math.e) / math.sqrt(128)) for u in project(mq, bias_q))
    keys = jnp.concatenate([unit(u, 1.0) for u in project(mk, bias_k)], axis=0)
    values = jnp.concatenate(project(mv, bias_v), axis=0)
    all_low = low_lanes((1024, LN))
    values_low = jnp.where(all_low, values, 1.0).astype(BF)
    values_high = jnp.where(all_low, 1.0, values).astype(BF)

    def attend(q, v):
        return dot(jnp.exp2(dot_t(q, keys)).astype(BF), v)

    side = low_lanes((256, LN))
    for core in range(2):
        at = slice(core * 256, core * 256 + 256)
        first = attend(q_low[at], values_low)
        second = attend(q_high[at], values_high)
        over = jnp.where(side, first, second)
        under = pltpu.roll(jnp.where(side, second, first), LN // 2, 1)
        shares = (over / under).astype(BF)
        for z in range(8):
            out_ref[z * 2 + core] = shares[z * 32 : z * 32 + 32]


def step_of(stamps_ref, step):
    width = jnp.full((16, LN), stamps_ref[step + 1] - stamps_ref[step], jnp.int32)
    return width.astype(F32) / 1000.0


def increments_kernel(at_ref, stamps_ref, shares_ref, lat_ref, out_ref, own_ref):
    step, side = at_ref[0], at_ref[1]
    velocity = jnp.sum(shares_ref[...].astype(F32), axis=0)
    size = step_of(stamps_ref, step)
    start = jnp.where(step == 0, pack_rows(lat_ref[0]), 0.0)
    for part in range(2):
        mine = velocity[part * 16 : part * 16 + 16]
        grown = size * mine
        grown = jnp.where(side == part, grown + start, grown).astype(BF)
        for peer in range(16):
            out_ref[peer * 2 + part] = grown
    own_ref[...] = jnp.where(side == 0, velocity[:16], velocity[16:])


def finish_kernel(at_ref, stamps_ref, terms_ref, own_ref, lat_ref, updated_ref, velocity_ref):
    step, side = at_ref[0], at_ref[1]
    own = own_ref[...]
    size = step_of(stamps_ref, step)
    other = terms_ref[step * 2 + 1 - side].astype(F32)
    start = jnp.where(step == 0, pack_rows(lat_ref[0]), 0.0)
    velocity = own + other / size
    updated = size * own + start + other
    for j in range(15):
        term = terms_ref[2 * j].astype(F32) + terms_ref[2 * j + 1].astype(F32)
        updated = updated + jnp.where(j < step, term, 0.0)
    for ref, value in ((updated_ref, updated), (velocity_ref, velocity)):
        ref[0, 0:16] = value[:, : LN // 2]
        ref[0, 16:32] = pltpu.roll(value, LN // 2, 1)[:, : LN // 2]


def condition_table(timesteps):
    shape = (32, 512)
    col = lax.broadcasted_iota(jnp.int32, shape, 1)
    row = lax.broadcasted_iota(jnp.int32, shape, 0)
    source = col // 16
    feature = ((source % 16) * 2 + source // 16) * 8 + col % 8
    half_count = 128
    place = (feature % half_count).astype(F32)
    frequencies = jnp.exp(-math.log(10000.0) * place / half_count)
    stamps = jnp.tile(timesteps[:16].astype(F32), 2)
    angles = stamps[:, None] * frequencies
    value = jnp.where(feature < half_count, jnp.cos(angles), jnp.sin(angles))
    return jnp.where(row // 16 == (col // 8) % 2, value, 0.0)


def call(kernel, out_shape, name, scalars, *args):
    smem = pl.BlockSpec(memory_space=SMEM)
    vmem = pl.BlockSpec(memory_space=pltpu.VMEM)
    return pl.pallas_call(
        kernel,
        in_specs=[smem] * len(scalars) + [vmem] * len(args),
        out_shape=out_shape,
        name=name,
    )(*scalars, *args)


def on_device(latents, timesteps, embed_weight, mod_weight, qkv_weight, out_weight):
    at = jnp.stack([lax.axis_index(STEP), lax.axis_index("y_hi")]).astype(jnp.int32)
    payload = pack(at, latents, mod_weight, 16)
    payload = lax.all_to_all(payload, ("z", "y_hi"), 0, 0, tiled=True)
    everything = lax.all_gather(payload, "core")
    table = condition_table(timesteps)
    w = jnp.moveaxis(qkv_weight[:, 0], 1, 0)
    centered, gram, wv = weights(at, embed_weight, w[2], out_weight)
    parts = call(
        partial_kernel,
        jax.ShapeDtypeStruct((16, 176, LN), BF),
        "partial",
        (),
        everything,
        table,
        centered,
        w,
        wv,
    )
    parts = lax.all_to_all(parts, STEP, 0, 0, tiled=True)
    shares = pl.pallas_call(
        attend_kernel,
        grid=(1,),
        in_specs=[
            pl.BlockSpec((16, 176, LN), lambda i: (0, 0, 0)),
            pl.BlockSpec((2, 16, 16, LN), lambda i: (0, 0, 0, 0)),
            pl.BlockSpec((2, LN, LN), lambda i: (0, 0, 0)),
        ],
        out_specs=pl.BlockSpec((16, 32, LN), lambda i: (0, 0, 0)),
        out_shape=jax.ShapeDtypeStruct((16, 32, LN), BF),
        name="attend",
    )(parts, everything, gram)
    shares = lax.all_to_all(shares, ("z", "core"), 0, 0, tiled=True)
    terms, own = call(
        increments_kernel,
        [jax.ShapeDtypeStruct((32, 16, LN), BF), jax.ShapeDtypeStruct((16, LN), F32)],
        "increments",
        (at, timesteps),
        shares,
        latents,
    )
    terms = lax.all_to_all(terms, ("y_lo", "x", "y_hi"), 0, 0, tiled=True)
    out = jax.ShapeDtypeStruct(latents.shape, F32)
    updated, velocity = call(
        finish_kernel, [out, out], "finish", (at, timesteps), terms, own, latents
    )
    return updated, velocity


def solution(mesh):
    split = Mesh(mesh.devices.reshape(4, 4, 8, 2, 2), STEP + SEQ)
    return jax.shard_map(
        on_device,
        mesh=split,
        in_specs=(
            P(STEP, SEQ, None),
            P(),
            P(),
            P(SEQ, None, None),
            P(STEP, SEQ, None, None),
            P(SEQ, None, None),
        ),
        out_specs=(P(STEP, SEQ, None), P(STEP, SEQ, None)),
        check_vma=False,
    )
```

time: 170 us -> 104 us (0.61)
  blocking collectives: 17.8 us -> 60.8 us
  waiting for transfers between devices: 42.4 us -> 5.47 us
  matrix products: 22.2 us -> 0 us
  starting transfers between devices: 36.2 us -> 16.2 us
  local copies, waits for them, and re-layouts: 22.7 us -> 2.93 us
  Pallas kernels: 0 us -> 15.9 us
  between operations: 15.6 us -> 0.69 us
  other arithmetic: 12.6 us -> 1.63 us
    all_to_all x0 -> x3, blocking collectives: none -> 56.5 us  [the longest x1 26.9 us: on_device(): parts = lax.all_to_all(parts, STEP, 0, 0, tiled=True)]
    all_to_all x4 -> x1, waiting for transfers between devices: 42.3 us -> 5.47 us  [on_device(): payload = lax.all_to_all(payload, ('z', 'y_hi'), 0, 0, tiled=True)]
    dot_general x8 -> x0, matrix products: 22.2 us -> none  [the longest x1 10.3 us: on_device(): jnp.dot(gathered, flat_piece, preferred_element_type=jnp.float32)]
    all_to_all x4 -> x1, starting transfers between devices: 36.2 us -> 16.2 us  [on_device(): payload = lax.all_to_all(payload, ('z', 'y_hi'), 0, 0, tiled=True)]
    pallas_call x0 -> x6, Pallas kernels: none -> 15.9 us  [the longest x3 6.39 us: call(): pl.pallas_call(kernel, in_specs=[smem] * len(scalars) + [vmem] * len(args...]
    all_gather x1, blocking collectives: 17.8 us -> 4.29 us  [on_device(): everything = lax.all_gather(payload, 'core')]
    reduce_sum x6 -> x0, other arithmetic: 8.32 us -> none  [the longest x1 7.54 us: modulate(): variance = jnp.mean(centered * centered, axis=-1, keepdims=True)]
    transpose x1 -> x0, local copies, waits for them, and re-layouts: 6.26 us -> none  [gather_in_order(): pieces = pieces.transpose(*back, *range(len(axes), pieces.ndim))]
  transfers between devices with their start and end apart: 5 -> 1, of which waited for: 4 -> 1; matrix products, arithmetic and copies ran while one was open for 13% -> 3% of each run, Pallas kernels for 0% -> 3%
where the time goes in v1:
time: 104 us
  blocking collectives  60.8 us (58%)
  starting transfers between devices  16.2 us (16%)
  Pallas kernels  15.9 us (15%)
  waiting for transfers between devices  5.47 us (5%)
  local copies, waits for them, and re-layouts  2.93 us (3%)
  other arithmetic  1.63 us (2%)
    all_to_all x1, blocking collectives, on_device(): parts = lax.all_to_all(parts, STEP, 0, 0, tiled=True)  26.9 us
    all_to_all x1, starting transfers between devices, on_device(): payload = lax.all_to_all(payload, ('z', 'y_hi'), 0, 0, tiled=True)  16.2 us
    all_to_all x1, blocking collectives, on_device(): shares = lax.all_to_all(shares, ('z', 'core'), 0, 0, tiled=True)  15.3 us
    all_to_all x1, blocking collectives, on_device(): terms = lax.all_to_all(terms, ('y_lo', 'x', 'y_hi'), 0, 0, tiled=True)  14.3 us
    pallas_call x3, Pallas kernels, call(): pl.pallas_call(kernel, in_specs=[smem] * len(scalars) + [vmem] * len(args...  6.39 us
    all_to_all x1, waiting for transfers between devices, on_device(): payload = lax.all_to_all(payload, ('z', 'y_hi'), 0, 0, tiled=True)  5.47 us
    all_gather x1, blocking collectives, on_device(): everything = lax.all_gather(payload, 'core')  4.29 us
    pallas_call x1, Pallas kernels, on_device(): pl.pallas_call(attend_kernel, grid=(1,), in_specs=[pl.BlockSpec((16, 176,...  3.71 us
  transfers between devices with their start and end apart: 1, of which 1 were waited for; matrix products, arithmetic and copies ran while one was open for 3% of the time, Pallas kernels for 3%

profile of v1, /device:TPU:1, one launch (start us, length us, event | category | flops | bytes accessed | tf_op | source)
XLA Modules:
  0.0 103.5 jit_solution(16500317966399213542)
XLA Ops:
  0.6 0.6 pad_add_fusion.at_ref
  1.2 2.2 %pack.1 = bf16[16,80,128]{2,1,0:T(8,128)(2,1)} custom-call(s32[2]{0:T(128)} %pad_add_fusion.at_ref, f32[1,32,64]{2,1,0:T(8,128)} %lat_ref.5, f32[8,2,4096]{2,1,0:T(2,128)} %mw_ref.1), custom_call_target="tpu_custom_call" | custom-call | tf_op jit(solution)/shard_map/pack/pallas_call | solution.py:57
  3.5 16.2 %all-to-all-start = ((bf16[16,80,128]{2,1,0:T(8,128)(2,1)}), bf16[16,80,128]{2,1,0:T(8,128)(2,1)S(1)}, u32[]{:S(2)}, u32[]{:S(2)}) async-start(bf16[16,80,128]{2,1,0:T(8,128)(2,1)} %pack.1), calls=%async_computation | async-start | bytes 655360 | tf_op jit(solution)/shard_map/all_to_all | solution.py:271
  19.7 0.0 copy-start.1
  19.7 0.6 copy-done.1
  20.4 0.0 copy-start
  20.4 1.5 %slice_bitcast_fusion.w_ref = bf16[256,128]{1,0:T(8,128)(2,1)} fusion(bf16[3,256,128]{2,1,0:T(8,128)(2,1)} %bitcast.10), kind=kLoop, calls=%fused_computation.30 | loop fusion | bytes 131072 | tf_op jit(solution)/shard_map/squeeze | solution.py:275
  21.9 0.1 mul.30
  21.9 0.0 copy-done
  21.9 0.7 copy.9.out_ref
  22.7 3.6 %weights.1 = (f32[64,256]{1,0:T(8,128)}, bf16[2,128,128]{2,1,0:T(8,128)(2,1)}, bf16[2,256,128]{2,1,0:T(8,128)(2,1)}) custom-call(s32[2]{0:T(128)} %pad_add_fusion.at_ref, bf16[64,4096]{1,0:T(8,128)(2,1)} %part_ref.1, bf16[64,4096]{1,0:T(8,128)(2,1)} %part_ref.1, bf16[256,128]{1,0:T(8,128)(2,1)} %slice_bitcast_fusion.w_ref, bf16[1,128,64]{2,1,0:T(8,128)(2,1)} %copy.9.out_ref), custom_call_target="tpu_custom_call" | custom-call | tf_op jit(solution)/shard_map/weights/pallas_call | solution.py:91
  26.2 1.0 select_select_fusion.2.cond_ref
  27.2 5.5 %all-to-all-done = bf16[16,80,128]{2,1,0:T(8,128)(2,1)S(1)} async-done(((bf16[16,80,128]{2,1,0:T(8,128)(2,1)}), bf16[16,80,128]{2,1,0:T(8,128)(2,1)S(1)}, u32[]{:S(2)}, u32[]{:S(2)}) %all-to-all-start) | async-done | bytes 327712 | tf_op jit(solution)/shard_map/all_to_all | solution.py:271
  32.7 4.3 %all-gather = bf16[32,80,128]{2,1,0:T(8,128)(2,1)} all-gather(bf16[16,80,128]{2,1,0:T(8,128)(2,1)S(1)} %all-to-all-done), channel_id=2, replica_groups=mesh['y_lo'=4,'x'=4,'z'=8,'y_hi'=2,'core'=2] {'core'}, dimensions={0}, use_global_device_ids=true | all-gather | bytes 983040 | tf_op jit(solution)/shard_map/all_gather | solution.py:272
  37.0 3.0 %partial.1 = bf16[16,176,128]{2,1,0:T(8,128)(2,1)} custom-call(bf16[2,16,80,128]{3,2,1,0:T(8,128)(2,1)} %bitcast.8, f32[32,512]{1,0:T(8,128)} %select_select_fusion.2.cond_ref, f32[64,256]{1,0:T(8,128)} %get-tuple-element.7.centered_ref, bf16[3,256,128]{2,1,0:T(8,128)(2,1)} %bitcast.11, bf16[2,256,128]{2,1,0:T(8,128)(2,1)} %get-tuple-element.8.wv_ref), custom_call_target="tpu_custom_call" | custom-call | tf_op jit(solution)/shard_map/partial/pallas_call | solution.py:260
  40.0 26.9 %all_to_all.20.parts_ref = bf16[16,176,128]{2,1,0:T(8,128)(2,1)} all-to-all(bf16[16,176,128]{2,1,0:T(8,128)(2,1)} %partial.1), channel_id=1, replica_groups=mesh['y_lo'=4,'x'=4,'z'=8,'y_hi'=2,'core'=2] {'y_lo','x'}, dimensions={0} | all-to-all | bytes 1441792 | tf_op jit(solution)/shard_map/all_to_all | solution.py:287
  66.9 3.7 %attend.1 = bf16[16,32,128]{2,1,0:T(8,128)(2,1)} custom-call(bf16[16,176,128]{2,1,0:T(8,128)(2,1)} %all_to_all.20.parts_ref, bf16[2,16,80,128]{3,2,1,0:T(8,128)(2,1)} %bitcast.9, bf16[2,128,128]{2,1,0:T(8,128)(2,1)} %get-tuple-element.9.gram_ref), custom_call_target="tpu_custom_call" | custom-call | tf_op jit(solution)/shard_map/attend/pallas_call | solution.py:288
  70.6 15.3 %all_to_all.21.shares_ref = bf16[16,32,128]{2,1,0:T(8,128)(2,1)} all-to-all(bf16[16,32,128]{2,1,0:T(8,128)(2,1)} %attend.1), channel_id=1, replica_groups=mesh['y_lo'=4,'x'=4,'z'=8,'y_hi'=2,'core'=2] {'z','core'}, dimensions={0} | all-to-all | bytes 262144 | tf_op jit(solution)/shard_map/all_to_all | solution.py:300
  85.9 1.6 %increments.1 = (bf16[32,16,128]{2,1,0:T(8,128)(2,1)}, f32[16,128]{1,0:T(8,128)}) custom-call(s32[2]{0:T(128)} %pad_add_fusion.at_ref, s32[17]{0:T(128)} %stamps_ref.3, bf16[16,32,128]{2,1,0:T(8,128)(2,1)} %all_to_all.21.shares_ref, f32[1,32,64]{2,1,0:T(8,128)} %lat_ref.5), custom_call_target="tpu_custom_call" | custom-call | tf_op jit(solution)/shard_map/increments/pallas_call | solution.py:260
  87.5 14.3 %all_to_all.22.terms_ref = bf16[32,16,128]{2,1,0:T(8,128)(2,1)} all-to-all(bf16[32,16,128]{2,1,0:T(8,128)(2,1)} %get-tuple-element.10), channel_id=1, replica_groups=mesh['y_lo'=4,'x'=4,'z'=8,'y_hi'=2,'core'=2] {'y_lo','x','y_hi'}, dimensions={0} | all-to-all | bytes 262144 | tf_op jit(solution)/shard_map/all_to_all | solution.py:309
  101.8 1.7 %finish.1 = (f32[1,32,64]{2,1,0:T(8,128)}, f32[1,32,64]{2,1,0:T(8,128)}) custom-call(s32[2]{0:T(128)} %pad_add_fusion.at_ref, s32[17]{0:T(128)} %stamps_ref.3, bf16[32,16,128]{2,1,0:T(8,128)(2,1)} %all_to_all.22.terms_ref, f32[16,128]{1,0:T(8,128)} %get-tuple-element.11.own_ref, f32[1,32,64]{2,1,0:T(8,128)} %lat_ref.5), custom_call_target="tpu_custom_call" | custom-call | tf_op jit(solution)/shard_map/finish/pallas_call | solution.py:260
  (9 shorter events, 0.0 us)
Async XLA Ops:
  3.5 29.2 %all-to-all-start = ((bf16[16,80,128]{2,1,0:T(8,128)(2,1)}), bf16[16,80,128]{2,1,0:T(8,128)(2,1)S(1)}, u32[]{:S(2)}, u32[]{:S(2)}) async-start(bf16[16,80,128]{2,1,0:T(8,128)(2,1)} %pack.1), calls=%async_computation | async-start | bytes 655360 | tf_op jit(solution)/shard_map/all_to_all | solution.py:271
  19.7 0.7 copy-start.1
  20.4 1.6 %copy-start = (bf16[1,128,64]{1,2,0:T(8,128)(2,1)S(1)}, bf16[1,128,64]{1,2,0:T(8,128)(2,1)}, u32[]{:S(2)}) copy-start(bf16[1,128,64]{1,2,0:T(8,128)(2,1)} %param.11) | copy-start | bytes 49156

commit v2 on v1

v2 whole, which is shorter than its diff:
```python
import math

import jax
import jax.numpy as jnp
from jax import lax
from jax.experimental import pallas as pl
from jax.experimental.pallas import tpu as pltpu
from jax.sharding import Mesh
from jax.sharding import PartitionSpec as P


STEP = ("y_lo", "x")
SEQ = ("z", "y_hi", "core")
BF = jnp.bfloat16
F32 = jnp.float32
LN = 128


def dot(a, b):
    return jnp.dot(a, b, preferred_element_type=F32)


def dot_t(a, b):
    return lax.dot_general(a, b, (((1,), (1,)), ((), ())), preferred_element_type=F32)


def halves(x):
    hi = x.astype(BF)
    return hi, (x - hi.astype(F32)).astype(BF)


def low_lanes(shape):
    return lax.broadcasted_iota(jnp.int32, shape, len(shape) - 1) < LN // 2


def pack_rows(rows):
    return jnp.concatenate([rows[:16], rows[16:]], axis=1)


def place(*axes):
    index = 0
    for axis in axes:
        index = index * lax.axis_size(axis) + lax.axis_index(axis)
    return index


def own_columns():
    return pl.ds(pl.multiple_of(place("y_lo") * 1024, 1024), 1024)


def conditions(stamps_ref):
    shape = (8, 16)
    row = lax.broadcasted_iota(jnp.int32, shape, 0)
    col = lax.broadcasted_iota(jnp.int32, shape, 1)
    stamp = jnp.zeros(shape, jnp.int32)
    for k in range(4):
        stamp = jnp.where(row % 4 == k, stamps_ref[k * 4 + place("x")], stamp)
    feature = place(*SEQ) * 8 + col % 8
    half_count = 128
    frequencies = jnp.exp(-math.log(10000.0) * (feature % half_count).astype(F32) / half_count)
    angles = stamp.astype(F32) * frequencies
    value = jnp.where(feature < half_count, jnp.cos(angles), jnp.sin(angles))
    return jnp.where(row // 4 == col // 8, value, 0.0)


def pack_kernel(stamps_ref, lat_ref, mw_ref, out_ref):
    lat = pack_rows(lat_ref[0]).astype(BF)
    own = own_columns()
    cond_hi, cond_lo = halves(conditions(stamps_ref))
    hi, lo = halves(jnp.concatenate([mw_ref[:, 0, own], mw_ref[:, 1, own]], axis=0))
    share = dot(cond_hi, hi) + dot(cond_lo, hi) + dot(cond_hi, lo)
    blocks = [share[:, part * LN : (part + 1) * LN] for part in range(8)]
    payload = jnp.concatenate([lat, jnp.concatenate(blocks, axis=0).astype(BF)], axis=0)
    for peer in range(out_ref.shape[0]):
        out_ref[peer] = payload


def weights_kernel(embed_ref, centered_ref, gram_ref):
    embed = embed_ref[...].astype(F32)
    mean = jnp.mean(embed, axis=1, keepdims=True)
    centered_ref[...] = embed_ref[:, own_columns()].astype(F32) - mean
    hi, lo = halves(embed - mean)
    hi2 = jnp.concatenate([hi, hi], axis=0)
    lo2 = jnp.concatenate([lo, lo], axis=0)
    gram = (dot_t(hi2, hi2) + dot_t(hi2, lo2) + dot_t(lo2, hi2)) * (1.0 / embed.shape[1])
    row = lax.broadcasted_iota(jnp.int32, gram.shape, 0) < LN // 2
    gram = jnp.where(row == low_lanes(gram.shape), gram, 0.0)
    gram_ref[0], gram_ref[1] = halves(gram)


def partial_kernel(mod_ref, centered_ref, out_weight_ref, *refs):
    w_refs, out_ref, modulation_ref = refs[:4], refs[4], refs[5]
    total = jnp.sum(mod_ref[:, 16:80, :].astype(F32), axis=0)
    for part in range(8):
        modulation_ref[:, part * LN : (part + 1) * LN] = total[part * 8 : part * 8 + 8]
    out = out_weight_ref[0]
    out = jnp.concatenate([out, out], axis=0)
    mq = mk = mv = 0.0
    biases = [0.0, 0.0, 0.0]
    for far, w_ref in enumerate(w_refs):
        origin = lax.rem(place("x") + 4 - far, 4)
        own = pl.ds(pl.multiple_of(origin * 256, 256), 256)
        modulation = modulation_ref[:, own]
        shift, scale = modulation[:4], modulation[4:] + 1.0
        centered = centered_ref[:, own]
        rows = jnp.concatenate(
            [(centered * scale[k : k + 1]).astype(BF) for k in range(4)], axis=0
        )
        shift2 = jnp.concatenate(halves(shift), axis=0)
        wq, wk, wv = w_ref[0:256], w_ref[256:512], w_ref[512:768]
        wv_hi, wv_lo = halves(dot_t(wv, out))
        mq = mq + dot(rows, wq)
        mk = mk + dot(rows, wk)
        mv = mv + dot(rows, wv_hi) + dot(rows, wv_lo)
        for j, w in enumerate((wq, wk, wv_hi)):
            b = dot(shift2, w)
            biases[j] = biases[j] + b[:4] + b[4:]
        biases[2] = biases[2] + dot(shift2, wv_lo)[:4]
    line = lax.broadcasted_iota(jnp.int32, (16, LN), 0)
    low = low_lanes((32, LN))
    for k in range(4):
        at = slice(k * 64, k * 64 + 64)
        out_ref[k, 0:64] = mq[at].astype(BF)
        out_ref[k, 64:128] = mk[at].astype(BF)
        v = mv[at]
        out_ref[k, 128:160] = jnp.where(low, v[:32], v[32:]).astype(BF)
        tile = jnp.where(line == 0, biases[0][k : k + 1], 0.0)
        tile = jnp.where(line == 1, biases[1][k : k + 1], tile)
        tile = jnp.where(line == 2, biases[2][k : k + 1], tile)
        out_ref[k, 160:176] = tile.astype(BF)


def attend_kernel(parts_ref, lat_ref, gram_ref, out_ref):
    total = jnp.sum(parts_ref[...].astype(F32), axis=0)
    mq, mk, mv = total[0:64], total[64:128], total[128:160]
    low32 = low_lanes((32, LN))
    turned = pltpu.roll(mv, LN // 2, 1)
    mv = jnp.concatenate(
        [jnp.where(low32, mv, turned), jnp.where(low32, turned, mv)], axis=0
    )
    bias_q, bias_k, bias_v = total[160:161], total[161:162], total[162:163]
    packed = lat_ref[:, 0:16, :].reshape(512, LN)
    as_float = packed.astype(F32)
    square = (dot(packed, gram_ref[0]) + dot(packed, gram_ref[1])) * as_float
    low = low_lanes((512, LN))
    gain_low = lax.rsqrt(jnp.sum(jnp.where(low, square, 0.0), axis=1, keepdims=True) + 1e-06)
    gain_high = lax.rsqrt(jnp.sum(jnp.where(low, 0.0, square), axis=1, keepdims=True) + 1e-06)
    twice = jnp.concatenate([packed, packed], axis=1)
    none = jnp.zeros((64, LN), BF)

    def project(m, bias):
        hi, lo = halves(m)
        first = dot(twice, jnp.concatenate([hi, none, lo, none], axis=0))
        second = dot(twice, jnp.concatenate([none, hi, none, lo], axis=0))
        return gain_low * first + bias, gain_high * second + bias

    def unit(u, factor):
        mean = jnp.mean(u * u, axis=1, keepdims=True)
        return (u * (lax.rsqrt(mean + 1e-06) * factor)).astype(BF)

    q_low, q_high = (unit(u, math.log2(math.e) / math.sqrt(128)) for u in project(mq, bias_q))
    keys = jnp.concatenate([unit(u, 1.0) for u in project(mk, bias_k)], axis=0)
    values = jnp.concatenate(project(mv, bias_v), axis=0)
    all_low = low_lanes((1024, LN))
    values_low = jnp.where(all_low, values, 1.0).astype(BF)
    values_high = jnp.where(all_low, 1.0, values).astype(BF)

    def attend(q, v):
        return dot(jnp.exp2(dot_t(q, keys)).astype(BF), v)

    side = low_lanes((256, LN))
    for core in range(2):
        at = slice(core * 256, core * 256 + 256)
        first = attend(q_low[at], values_low)
        second = attend(q_high[at], values_high)
        over = jnp.where(side, first, second)
        under = pltpu.roll(jnp.where(side, second, first), LN // 2, 1)
        shares = (over / under).astype(BF)
        for z in range(8):
            out_ref[z * 2 + core] = shares[z * 32 : z * 32 + 32]


def step_of(stamps_ref, step):
    width = jnp.full((16, LN), stamps_ref[step + 1] - stamps_ref[step], jnp.int32)
    return width.astype(F32) / 1000.0


def increments_kernel(stamps_ref, shares_ref, lat_ref, out_ref, own_ref):
    step, side = place(*STEP), place("y_hi")
    velocity = jnp.sum(shares_ref[...].astype(F32), axis=0)
    size = step_of(stamps_ref, step)
    start = jnp.where(step == 0, pack_rows(lat_ref[0]), 0.0)
    for part in range(2):
        mine = velocity[part * 16 : part * 16 + 16]
        grown = size * mine
        grown = jnp.where(side == part, grown + start, grown).astype(BF)
        for peer in range(16):
            out_ref[peer * 2 + part] = grown
    own_ref[...] = jnp.where(side == 0, velocity[:16], velocity[16:])


def finish_kernel(stamps_ref, terms_ref, own_ref, lat_ref, updated_ref, velocity_ref):
    step, side = place(*STEP), place("y_hi")
    own = own_ref[...]
    size = step_of(stamps_ref, step)
    other = terms_ref[step * 2 + 1 - side].astype(F32)
    start = jnp.where(step == 0, pack_rows(lat_ref[0]), 0.0)
    velocity = own + other / size
    updated = size * own + start + other
    for j in range(15):
        term = terms_ref[2 * j].astype(F32) + terms_ref[2 * j + 1].astype(F32)
        updated = updated + jnp.where(j < step, term, 0.0)
    for ref, value in ((updated_ref, updated), (velocity_ref, velocity)):
        ref[0, 0:16] = value[:, : LN // 2]
        ref[0, 16:32] = pltpu.roll(value, LN // 2, 1)[:, : LN // 2]


def near(x):
    return pltpu.with_memory_space_constraint(x, pltpu.VMEM)


def call(kernel, outs, *args, scalars=(), scratch=()):
    smem = pl.BlockSpec(memory_space=pltpu.SMEM)
    vmem = pl.BlockSpec(memory_space=pltpu.VMEM)
    return pl.pallas_call(
        kernel,
        in_specs=[smem] * len(scalars) + [vmem] * len(args),
        out_specs=[vmem] * len(outs),
        out_shape=outs,
        scratch_shapes=scratch,
    )(*scalars, *args)


def stages(latents, timesteps, embed_weight, mod_weight, qkv_weight, out_weight):
    vmem = pltpu.VMEM
    (payload,) = call(
        pack_kernel, [vmem((16, 80, LN), BF)], latents, mod_weight, scalars=(timesteps,)
    )
    payload = lax.all_to_all(payload, ("z", "y_hi"), 0, 0, tiled=True)
    gathered = near(lax.all_gather(payload, "core", tiled=True))
    w = jnp.moveaxis(qkv_weight[:, 0], 1, 0).reshape(768, LN)
    ws = [w] + [lax.ppermute(w, "x", [(i, (i + far) % 4) for i in range(4)]) for far in (1, 2, 3)]
    centered, gram = call(
        weights_kernel, [vmem((64, 1024), F32), vmem((2, LN, LN), BF)], embed_weight
    )
    (parts,) = call(
        partial_kernel,
        [vmem((4, 176, LN), BF)],
        gathered,
        near(centered),
        near(jnp.swapaxes(out_weight, 1, 2)),
        *[near(w) for w in ws],
        scratch=[vmem((8, 1024), F32)],
    )
    parts = near(lax.all_to_all(parts, "y_lo", 0, 0, tiled=True))
    (shares,) = call(attend_kernel, [vmem((16, 32, LN), BF)], parts, gathered, near(gram))
    shares = near(lax.all_to_all(shares, ("z", "core"), 0, 0, tiled=True))
    terms, own = call(
        increments_kernel,
        [vmem((32, 16, LN), BF), vmem((16, LN), F32)],
        shares,
        latents,
        scalars=(timesteps,),
    )
    terms = near(lax.all_to_all(terms, ("y_lo", "x", "y_hi"), 0, 0, tiled=True))
    out = jax.ShapeDtypeStruct(latents.shape, F32)
    return tuple(
        call(finish_kernel, [out, out], terms, near(own), latents, scalars=(timesteps,))
    )


def solution(mesh):
    split = Mesh(mesh.devices.reshape(4, 4, 8, 2, 2), STEP + SEQ)
    return jax.shard_map(
        stages,
        mesh=split,
        in_specs=(
            P(STEP, SEQ, None),
            P(),
            P(),
            P(SEQ, None, None),
            P(STEP, SEQ, None, None),
            P(SEQ, None, None),
        ),
        out_specs=(P(STEP, SEQ, None), P(STEP, SEQ, None)),
        check_vma=False,
    )
```

time: 104 us -> 85.6 us (0.82)
  blocking collectives: 60.8 us -> 46.1 us
  starting transfers between devices: 16.2 us -> 25.7 us
  Pallas kernels: 15.9 us -> 9.73 us
  waiting for transfers between devices: 5.47 us -> 2.41 us
  local copies, waits for them, and re-layouts: 2.93 us -> 0.01 us
  other arithmetic: 1.63 us -> 0 us
    all_to_all x3, blocking collectives: 56.5 us -> 41.9 us  [the longest x1 16.1 us: stages(): terms = near(lax.all_to_all(terms, ('y_lo', 'x', 'y_hi'), 0, 0, tiled=True))]
    pallas_call x3 -> x0, Pallas kernels: 9.47 us -> none  [the longest x1 3.71 us: on_device(): pl.pallas_call(attend_kernel, grid=(1,), in_specs=[pl.BlockSpec((16, 176,...]
    ppermute x0 -> x3, starting transfers between devices: none -> 9.33 us  [stages(): lax.ppermute(w, 'x', [(i, (i + far) % 4) for i in range(4)])]
    all_to_all x1, waiting for transfers between devices: 5.47 us -> 1.44 us  [stages(): payload = lax.all_to_all(payload, ('z', 'y_hi'), 0, 0, tiled=True)]
    pallas_call x3 -> x6, Pallas kernels: 6.39 us -> 9.73 us  [call(): pl.pallas_call(kernel, in_specs=[smem] * len(scalars) + [vmem] * len(args...]
    squeeze x1 -> x0, local copies, waits for them, and re-layouts: 1.48 us -> none  [on_device(): centered, gram, wv = weights(at, embed_weight, w[2], out_weight)]
    unnamed x5 -> x4, local copies, waits for them, and re-layouts: 1.36 us -> 0.01 us
  transfers between devices with their start and end apart: 1 -> 4, of which waited for: 1 -> 2; matrix products, arithmetic and copies ran while one was open for 3% -> 0% of each run, Pallas kernels for 3% -> 3%
where the time goes in v2:
time: 85.6 us; the launch traced here: 84.6 us
  blocking collectives  46.1 us (54%)
  starting transfers between devices  25.7 us (30%)
  Pallas kernels  9.73 us (11%)
  waiting for transfers between devices  2.41 us (3%)
    all_to_all x1, starting transfers between devices, stages(): payload = lax.all_to_all(payload, ('z', 'y_hi'), 0, 0, tiled=True)  16.4 us
    all_to_all x1, blocking collectives, stages(): terms = near(lax.all_to_all(terms, ('y_lo', 'x', 'y_hi'), 0, 0, tiled=True))  16.1 us
    all_to_all x1, blocking collectives, stages(): shares = near(lax.all_to_all(shares, ('z', 'core'), 0, 0, tiled=True))  16 us
    all_to_all x1, blocking collectives, stages(): parts = near(lax.all_to_all(parts, 'y_lo', 0, 0, tiled=True))  9.86 us
    pallas_call x6, Pallas kernels, call(): pl.pallas_call(kernel, in_specs=[smem] * len(scalars) + [vmem] * len(args...  9.73 us
    ppermute x3, starting transfers between devices, stages(): lax.ppermute(w, 'x', [(i, (i + far) % 4) for i in range(4)])  9.33 us
    all_gather x1, blocking collectives, stages(): gathered = near(lax.all_gather(payload, 'core', tiled=True))  4.16 us
  transfers between devices with their start and end apart: 4, of which 2 were waited for; matrix products, arithmetic and copies ran while one was open for 0% of the time, Pallas kernels for 3%

profile of v2, /device:TPU:1, one launch (start us, length us, event | category | flops | bytes accessed | tf_op | source)
XLA Modules:
  0.0 84.6 jit_solution(16745813625933894494)
XLA Ops:
  0.6 1.9 %shard_map.77 = bf16[16,80,128]{2,1,0:T(8,128)(2,1)} custom-call(s32[17]{0:T(128)} %stamps_ref.5, f32[1,32,64]{2,1,0:T(8,128)} %lat_ref.5, f32[8,2,4096]{2,1,0:T(2,128)} %mw_ref.1), custom_call_target="tpu_custom_call" | custom-call | tf_op jit(solution)/shard_map/pallas_call | solution.py:225
  2.6 0.0 copy-start
  2.6 16.4 %all-to-all-start = ((bf16[16,80,128]{2,1,0:T(8,128)(2,1)}), bf16[16,80,128]{2,1,0:T(8,128)(2,1)S(1)}, u32[]{:S(2)}, u32[]{:S(2)}) async-start(bf16[16,80,128]{2,1,0:T(8,128)(2,1)} %shard_map.77), calls=%async_computation | async-start | bytes 655360 | tf_op jit(solution)/shard_map/all_to_all | solution.py:239
  18.9 0.0 copy-done
  18.9 4.4 %collective-permute-start.2 = (bf16[768,128]{1,0:T(8,128)(2,1)S(1)}, bf16[768,128]{1,0:T(8,128)(2,1)S(1)}, u32[]{:S(2)}, u32[]{:S(2)}) collective-permute-start(bf16[768,128]{1,0:T(8,128)(2,1)S(1)} %bitcast.6), channel_id=1, source_target_pairs={{0,96},{32,0},{64,32},{96,64},{1,97},{33,1},{65,33},{97,65},{2,98}... | collective-permute-start | bytes 589832 | tf_op jit(solution)/shard_map/ppermute | solution.py:242
  23.3 2.4 %collective-permute-start.1 = (bf16[768,128]{1,0:T(8,128)(2,1)S(1)}, bf16[768,128]{1,0:T(8,128)(2,1)S(1)}, u32[]{:S(2)}, u32[]{:S(2)}) collective-permute-start(bf16[768,128]{1,0:T(8,128)(2,1)S(1)} %bitcast.7), channel_id=1, source_target_pairs={{0,64},{32,96},{64,0},{96,32},{1,65},{33,97},{65,1},{97,33},{2,66}... | collective-permute-start | bytes 589832 | tf_op jit(solution)/shard_map/ppermute | solution.py:242
  25.8 2.5 %collective-permute-start = (bf16[768,128]{1,0:T(8,128)(2,1)S(1)}, bf16[768,128]{1,0:T(8,128)(2,1)S(1)}, u32[]{:S(2)}, u32[]{:S(2)}) collective-permute-start(bf16[768,128]{1,0:T(8,128)(2,1)S(1)} %bitcast.8), channel_id=1, source_target_pairs={{0,32},{32,64},{64,96},{96,0},{1,33},{33,65},{65,97},{97,1},{2,34}... | collective-permute-start | bytes 589832 | tf_op jit(solution)/shard_map/ppermute | solution.py:242
  28.3 2.2 %shard_map.78 = (f32[64,1024]{1,0:T(8,128)S(1)}, bf16[2,128,128]{2,1,0:T(8,128)(2,1)S(1)}) custom-call(bf16[64,4096]{1,0:T(8,128)(2,1)} %embed_ref.1), custom_call_target="tpu_custom_call" | custom-call | tf_op jit(solution)/shard_map/pallas_call | solution.py:225
  30.5 0.0 copy-start.1
  30.5 1.4 %all-to-all-done = bf16[16,80,128]{2,1,0:T(8,128)(2,1)S(1)} async-done(((bf16[16,80,128]{2,1,0:T(8,128)(2,1)}), bf16[16,80,128]{2,1,0:T(8,128)(2,1)S(1)}, u32[]{:S(2)}, u32[]{:S(2)}) %all-to-all-start) | async-done | bytes 327712 | tf_op jit(solution)/shard_map/all_to_all | solution.py:239
  32.0 4.2 %all_gather.3.mod_ref.lat_ref = bf16[32,80,128]{2,1,0:T(8,128)(2,1)S(1)} all-gather(bf16[16,80,128]{2,1,0:T(8,128)(2,1)S(1)} %all-to-all-done), channel_id=1, replica_groups=mesh['y_lo'=4,'x'=4,'z'=8,'y_hi'=2,'core'=2] {'core'}, dimensions={0}, use_global_device_ids=true | all-gather | bytes 983040 | tf_op jit(solution)/shard_map/all_gather | solution.py:240
  36.1 0.0 collective-permute-done.2.refs_3_
  36.1 0.0 collective-permute-done.1.refs_2_
  36.1 1.0 %collective-permute-done.refs_1_ = bf16[768,128]{1,0:T(8,128)(2,1)S(1)} collective-permute-done((bf16[768,128]{1,0:T(8,128)(2,1)S(1)}, bf16[768,128]{1,0:T(8,128)(2,1)S(1)}, u32[]{:S(2)}, u32[]{:S(2)}) %collective-permute-start) | collective-permute-done | bytes 196640 | tf_op jit(solution)/shard_map/ppermute | solution.py:242
  37.1 0.0 copy-done.1
  37.1 1.4 %shard_map.79 = bf16[4,176,128]{2,1,0:T(8,128)(2,1)S(1)} custom-call(bf16[32,80,128]{2,1,0:T(8,128)(2,1)S(1)} %all_gather.3.mod_ref.lat_ref, f32[64,1024]{1,0:T(8,128)S(1)} %get-tuple-element.6.centered_ref, bf16[1,64,128]{2,1,0:T(8,128)(2,1)S(1)} %bitcast.10, bf16[768,128]{1,0:T(8,128)(2,1)S(1)} %bitcast.9, ...), custom_call_target="tpu_custom_call" | custom-call | tf_op jit(solution)/shard_map/pallas_call | solution.py:225
  38.4 9.9 %all_to_all.20.parts_ref = bf16[4,176,128]{2,1,0:T(8,128)(2,1)S(1)} all-to-all(bf16[4,176,128]{2,1,0:T(8,128)(2,1)S(1)} %shard_map.79), channel_id=1, replica_groups=mesh['y_lo'=4,'x'=4,'z'=8,'y_hi'=2,'core'=2] {'y_lo'}, dimensions={0} | all-to-all | bytes 360448 | tf_op jit(solution)/shard_map/all_to_all | solution.py:255
  48.3 1.9 %shard_map.80 = bf16[16,32,128]{2,1,0:T(8,128)(2,1)S(1)} custom-call(bf16[4,176,128]{2,1,0:T(8,128)(2,1)S(1)} %all_to_all.20.parts_ref, bf16[32,80,128]{2,1,0:T(8,128)(2,1)S(1)} %all_gather.3.mod_ref.lat_ref, bf16[2,128,128]{2,1,0:T(8,128)(2,1)S(1)} %get-tuple-element.7.gram_ref), custom_call_target="tpu_custom_call" | custom-call | tf_op jit(solution)/shard_map/pallas_call | solution.py:225
  50.2 16.0 %all_to_all.21.shares_ref = bf16[16,32,128]{2,1,0:T(8,128)(2,1)S(1)} all-to-all(bf16[16,32,128]{2,1,0:T(8,128)(2,1)S(1)} %shard_map.80), channel_id=1, replica_groups=mesh['y_lo'=4,'x'=4,'z'=8,'y_hi'=2,'core'=2] {'z','core'}, dimensions={0} | all-to-all | bytes 262144 | tf_op jit(solution)/shard_map/all_to_all | solution.py:257
  66.2 0.8 shard_map.81
  67.0 16.1 %all_to_all.22.terms_ref = bf16[32,16,128]{2,1,0:T(8,128)(2,1)S(1)} all-to-all(bf16[32,16,128]{2,1,0:T(8,128)(2,1)S(1)} %get-tuple-element.8), channel_id=1, replica_groups=mesh['y_lo'=4,'x'=4,'z'=8,'y_hi'=2,'core'=2] {'y_lo','x','y_hi'}, dimensions={0} | all-to-all | bytes 262144 | tf_op jit(solution)/shard_map/all_to_all | solution.py:265
  83.1 1.5 %shard_map.82 = (f32[1,32,64]{2,1,0:T(8,128)}, f32[1,32,64]{2,1,0:T(8,128)}) custom-call(s32[17]{0:T(128)} %stamps_ref.5, bf16[32,16,128]{2,1,0:T(8,128)(2,1)S(1)} %all_to_all.22.terms_ref, f32[16,128]{1,0:T(8,128)S(1)} %get-tuple-element.9.own_ref, f32[1,32,64]{2,1,0:T(8,128)} %lat_ref.5), custom_call_target="tpu_custom_call" | custom-call | tf_op jit(solution)/shard_map/pallas_call | solution.py:225
Async XLA Ops:
  2.6 16.4 %copy-start = (bf16[256,1,3,128]{3,0,2,1:T(8,128)(2,1)S(1)}, bf16[256,1,3,128]{3,0,2,1:T(8,128)(2,1)}, u32[]{:S(2)}) copy-start(bf16[256,1,3,128]{3,0,2,1:T(8,128)(2,1)} %param.10) | copy-start | bytes 589828
  2.6 29.4 %all-to-all-start = ((bf16[16,80,128]{2,1,0:T(8,128)(2,1)}), bf16[16,80,128]{2,1,0:T(8,128)(2,1)S(1)}, u32[]{:S(2)}, u32[]{:S(2)}) async-start(bf16[16,80,128]{2,1,0:T(8,128)(2,1)} %shard_map.77), calls=%async_computation | async-start | bytes 655360 | tf_op jit(solution)/shard_map/all_to_all | solution.py:239
  18.9 17.2 %collective-permute-start.2 = (bf16[768,128]{1,0:T(8,128)(2,1)S(1)}, bf16[768,128]{1,0:T(8,128)(2,1)S(1)}, u32[]{:S(2)}, u32[]{:S(2)}) collective-permute-start(bf16[768,128]{1,0:T(8,128)(2,1)S(1)} %bitcast.6), channel_id=1, source_target_pairs={{0,96},{32,0},{64,32},{96,64},{1,97},{33,1},{65,33},{97,65},{2,98}... | collective-permute-start | bytes 589832 | tf_op jit(solution)/shard_map/ppermute | solution.py:242
  23.3 12.8 %collective-permute-start.1 = (bf16[768,128]{1,0:T(8,128)(2,1)S(1)}, bf16[768,128]{1,0:T(8,128)(2,1)S(1)}, u32[]{:S(2)}, u32[]{:S(2)}) collective-permute-start(bf16[768,128]{1,0:T(8,128)(2,1)S(1)} %bitcast.7), channel_id=1, source_target_pairs={{0,64},{32,96},{64,0},{96,32},{1,65},{33,97},{65,1},{97,33},{2,66}... | collective-permute-start | bytes 589832 | tf_op jit(solution)/shard_map/ppermute | solution.py:242
  25.8 11.3 %collective-permute-start = (bf16[768,128]{1,0:T(8,128)(2,1)S(1)}, bf16[768,128]{1,0:T(8,128)(2,1)S(1)}, u32[]{:S(2)}, u32[]{:S(2)}) collective-permute-start(bf16[768,128]{1,0:T(8,128)(2,1)S(1)} %bitcast.8), channel_id=1, source_target_pairs={{0,32},{32,64},{64,96},{96,0},{1,33},{33,65},{65,97},{97,1},{2,34}... | collective-permute-start | bytes 589832 | tf_op jit(solution)/shard_map/ppermute | solution.py:242
  30.5 6.6 %copy-start.1 = (bf16[1,128,64]{1,2,0:T(8,128)(2,1)S(1)}, bf16[1,128,64]{1,2,0:T(8,128)(2,1)}, u32[]{:S(2)}) copy-start(bf16[1,128,64]{1,2,0:T(8,128)(2,1)} %param.11) | copy-start | bytes 49156

commit v3 on v2

--- a/solution.py
+++ b/solution.py
@@ -63,7 +63,17 @@
     return jnp.where(row // 4 == col // 8, value, 0.0)
 
 
-def pack_kernel(stamps_ref, lat_ref, mw_ref, out_ref):
+def twin(lines):
+    low = low_lanes(lines.shape)
+    turned = pltpu.roll(lines, LN // 2, 1)
+    return jnp.concatenate([jnp.where(low, lines, turned), jnp.where(low, turned, lines)], axis=0)
+
+
+def pack_kernel(stamps_ref, lat_ref, mw_ref, w_ref, out_weight_ref, out_ref, folded_ref):
+    out = out_weight_ref[0]
+    wv = dot_t(w_ref[2], jnp.concatenate([out, out], axis=0))
+    folded_ref[0:512] = w_ref[0:2].reshape(512, LN)
+    folded_ref[512:640] = jnp.where(low_lanes((LN, LN)), wv[:LN], wv[LN:]).astype(BF)
     lat = pack_rows(lat_ref[0]).astype(BF)
     own = own_columns()
     cond_hi, cond_lo = halves(conditions(stamps_ref))
@@ -80,21 +90,21 @@
     mean = jnp.mean(embed, axis=1, keepdims=True)
     centered_ref[...] = embed_ref[:, own_columns()].astype(F32) - mean
     hi, lo = halves(embed - mean)
-    hi2 = jnp.concatenate([hi, hi], axis=0)
-    lo2 = jnp.concatenate([lo, lo], axis=0)
-    gram = (dot_t(hi2, hi2) + dot_t(hi2, lo2) + dot_t(lo2, hi2)) * (1.0 / embed.shape[1])
-    row = lax.broadcasted_iota(jnp.int32, gram.shape, 0) < LN // 2
-    gram = jnp.where(row == low_lanes(gram.shape), gram, 0.0)
+    products = dot_t(jnp.concatenate([hi, lo], axis=0), hi)
+    cross = products[64:]
+    gram = (products[:64] + cross + cross.T) * (1.0 / embed.shape[1])
+    none = jnp.zeros_like(gram)
+    gram = jnp.concatenate(
+        [jnp.concatenate([gram, none], axis=1), jnp.concatenate([none, gram], axis=1)], axis=0
+    )
     gram_ref[0], gram_ref[1] = halves(gram)
 
 
-def partial_kernel(mod_ref, centered_ref, out_weight_ref, *refs):
+def partial_kernel(mod_ref, centered_ref, *refs):
     w_refs, out_ref, modulation_ref = refs[:4], refs[4], refs[5]
     total = jnp.sum(mod_ref[:, 16:80, :].astype(F32), axis=0)
     for part in range(8):
         modulation_ref[:, part * LN : (part + 1) * LN] = total[part * 8 : part * 8 + 8]
-    out = out_weight_ref[0]
-    out = jnp.concatenate([out, out], axis=0)
     mq = mk = mv = 0.0
     biases = [0.0, 0.0, 0.0]
     for far, w_ref in enumerate(w_refs):
@@ -107,15 +117,14 @@
             [(centered * scale[k : k + 1]).astype(BF) for k in range(4)], axis=0
         )
         shift2 = jnp.concatenate(halves(shift), axis=0)
-        wq, wk, wv = w_ref[0:256], w_ref[256:512], w_ref[512:768]
-        wv_hi, wv_lo = halves(dot_t(wv, out))
+        wq, wk = w_ref[0:256], w_ref[256:512]
+        wv = twin(w_ref[512:640].astype(F32)).astype(BF)
         mq = mq + dot(rows, wq)
         mk = mk + dot(rows, wk)
-        mv = mv + dot(rows, wv_hi) + dot(rows, wv_lo)
-        for j, w in enumerate((wq, wk, wv_hi)):
+        mv = mv + dot(rows, wv)
+        for j, w in enumerate((wq, wk, wv)):
             b = dot(shift2, w)
             biases[j] = biases[j] + b[:4] + b[4:]
-        biases[2] = biases[2] + dot(shift2, wv_lo)[:4]
     line = lax.broadcasted_iota(jnp.int32, (16, LN), 0)
     low = low_lanes((32, LN))
     for k in range(4):
@@ -133,11 +142,7 @@
 def attend_kernel(parts_ref, lat_ref, gram_ref, out_ref):
     total = jnp.sum(parts_ref[...].astype(F32), axis=0)
     mq, mk, mv = total[0:64], total[64:128], total[128:160]
-    low32 = low_lanes((32, LN))
-    turned = pltpu.roll(mv, LN // 2, 1)
-    mv = jnp.concatenate(
-        [jnp.where(low32, mv, turned), jnp.where(low32, turned, mv)], axis=0
-    )
+    mv = twin(mv)
     bias_q, bias_k, bias_v = total[160:161], total[161:162], total[162:163]
     packed = lat_ref[:, 0:16, :].reshape(512, LN)
     as_float = packed.astype(F32)
@@ -215,6 +220,10 @@
         ref[0, 16:32] = pltpu.roll(value, LN // 2, 1)[:, : LN // 2]
 
 
+def over_x(w, far):
+    return lax.ppermute(w, "x", [(i, (i + far) % 4) for i in range(4)])
+
+
 def near(x):
     return pltpu.with_memory_space_constraint(x, pltpu.VMEM)
 
@@ -233,23 +242,29 @@
 
 def stages(latents, timesteps, embed_weight, mod_weight, qkv_weight, out_weight):
     vmem = pltpu.VMEM
-    (payload,) = call(
-        pack_kernel, [vmem((16, 80, LN), BF)], latents, mod_weight, scalars=(timesteps,)
+    payload, w = call(
+        pack_kernel,
+        [vmem((16, 80, LN), BF), vmem((640, LN), BF)],
+        latents,
+        mod_weight,
+        jnp.moveaxis(qkv_weight[:, 0], 1, 0),
+        jnp.swapaxes(out_weight, 1, 2),
+        scalars=(timesteps,),
     )
     payload = lax.all_to_all(payload, ("z", "y_hi"), 0, 0, tiled=True)
     gathered = near(lax.all_gather(payload, "core", tiled=True))
-    w = jnp.moveaxis(qkv_weight[:, 0], 1, 0).reshape(768, LN)
-    ws = [w] + [lax.ppermute(w, "x", [(i, (i + far) % 4) for i in range(4)]) for far in (1, 2, 3)]
+    ws = {2: over_x(w, 2)}
+    ws.update({far: over_x(w, far) for far in (1, 3)})
     centered, gram = call(
-        weights_kernel, [vmem((64, 1024), F32), vmem((2, LN, LN), BF)], embed_weight
+        weights_kernel, [vmem((64, 1024), F32), vmem((2, LN, LN), BF)], near(embed_weight)
     )
     (parts,) = call(
         partial_kernel,
         [vmem((4, 176, LN), BF)],
         gathered,
         near(centered),
-        near(jnp.swapaxes(out_weight, 1, 2)),
-        *[near(w) for w in ws],
+        near(w),
+        *[near(ws[far]) for far in (1, 2, 3)],
         scratch=[vmem((8, 1024), F32)],
     )
     parts = near(lax.all_to_all(parts, "y_lo", 0, 0, tiled=True))
@@ -259,13 +274,13 @@
         increments_kernel,
         [vmem((32, 16, LN), BF), vmem((16, LN), F32)],
         shares,
-        latents,
+        near(latents),
         scalars=(timesteps,),
     )
     terms = near(lax.all_to_all(terms, ("y_lo", "x", "y_hi"), 0, 0, tiled=True))
     out = jax.ShapeDtypeStruct(latents.shape, F32)
     return tuple(
-        call(finish_kernel, [out, out], terms, near(own), latents, scalars=(timesteps,))
+        call(finish_kernel, [out, out], terms, near(own), near(latents), scalars=(timesteps,))
     )
 
 

time: 85.6 us -> 83.6 us (0.977)
  Pallas kernels: 9.73 us -> 7.72 us
  starting transfers between devices: 25.7 us -> 26.8 us
    all_to_all x1, blocking collectives: 16 us -> 13.9 us  [stages(): shares = near(lax.all_to_all(shares, ('z', 'core'), 0, 0, tiled=True))]
    pallas_call x6, Pallas kernels: 9.73 us -> 7.72 us  [call(): pl.pallas_call(kernel, in_specs=[smem] * len(scalars) + [vmem] * len(args...]
    ppermute x3, starting transfers between devices: 9.33 us -> 10.5 us  [over_x(): return lax.ppermute(w, 'x', [(i, (i + far) % 4) for i in range(4)])]
    ppermute x3, waiting for transfers between devices: 0.97 us -> 0.01 us  [over_x(): return lax.ppermute(w, 'x', [(i, (i + far) % 4) for i in range(4)])]
    all_to_all x1, blocking collectives: 9.86 us -> 10.8 us  [stages(): parts = near(lax.all_to_all(parts, 'y_lo', 0, 0, tiled=True))]
    all_to_all x1, blocking collectives: 16.1 us -> 17 us  [stages(): terms = near(lax.all_to_all(terms, ('y_lo', 'x', 'y_hi'), 0, 0, tiled=True))]
  transfers between devices with their start and end apart: 4 -> 4, of which waited for: 2 -> 1; matrix products, arithmetic and copies ran while one was open for 0% -> 0% of each run, Pallas kernels for 3% -> 1%
where the time goes in v3:
time: 83.6 us; the launch traced here: 82.7 us
  blocking collectives  45.9 us (55%)
  starting transfers between devices  26.8 us (32%)
  Pallas kernels  7.72 us (9%)
  waiting for transfers between devices  1.65 us (2%)
    all_to_all x1, blocking collectives, stages(): terms = near(lax.all_to_all(terms, ('y_lo', 'x', 'y_hi'), 0, 0, tiled=True))  17 us
    all_to_all x1, starting transfers between devices, stages(): payload = lax.all_to_all(payload, ('z', 'y_hi'), 0, 0, tiled=True)  16.2 us
    all_to_all x1, blocking collectives, stages(): shares = near(lax.all_to_all(shares, ('z', 'core'), 0, 0, tiled=True))  13.9 us
    all_to_all x1, blocking collectives, stages(): parts = near(lax.all_to_all(parts, 'y_lo', 0, 0, tiled=True))  10.8 us
    ppermute x3, starting transfers between devices, over_x(): return lax.ppermute(w, 'x', [(i, (i + far) % 4) for i in range(4)])  10.5 us
    pallas_call x6, Pallas kernels, call(): pl.pallas_call(kernel, in_specs=[smem] * len(scalars) + [vmem] * len(args...  7.72 us
    all_gather x1, blocking collectives, stages(): gathered = near(lax.all_gather(payload, 'core', tiled=True))  4.16 us
  transfers between devices with their start and end apart: 4, of which 1 were waited for; matrix products, arithmetic and copies ran while one was open for 0% of the time, Pallas kernels for 1%

profile of v3, /device:TPU:1, one launch (start us, length us, event | category | flops | bytes accessed | tf_op | source)
XLA Modules:
  0.0 82.7 jit_solution(9664491082173799714)
XLA Ops:
  0.6 0.0 copy-start
  0.6 2.1 %shard_map.77 = (bf16[16,80,128]{2,1,0:T(8,128)(2,1)}, bf16[640,128]{1,0:T(8,128)(2,1)S(1)}) custom-call(s32[17]{0:T(128)} %stamps_ref.5, f32[1,32,64]{2,1,0:T(8,128)} %lat_ref.5, f32[8,2,4096]{2,1,0:T(2,128)} %mw_ref.1, bf16[3,256,128]{2,1,0:T(8,128)(2,1)} %bitcast.4, bf16[1,64,128]{2,1,0:T(8,128)(2,1)} %bitcast.5), custom_call_target="tpu_custom_call" | custom-call | tf_op jit(solution)/shard_map/pallas_call | solution.py:234
  2.7 16.2 %all-to-all-start = ((bf16[16,80,128]{2,1,0:T(8,128)(2,1)}), bf16[16,80,128]{2,1,0:T(8,128)(2,1)S(1)}, u32[]{:S(2)}, u32[]{:S(2)}) async-start(bf16[16,80,128]{2,1,0:T(8,128)(2,1)} %get-tuple-element.8), calls=%async_computation | async-start | bytes 655360 | tf_op jit(solution)/shard_map/all_to_all | solution.py:254
  18.9 3.1 %collective-permute-start = (bf16[640,128]{1,0:T(8,128)(2,1)S(1)}, bf16[640,128]{1,0:T(8,128)(2,1)S(1)}, u32[]{:S(2)}, u32[]{:S(2)}) collective-permute-start(bf16[640,128]{1,0:T(8,128)(2,1)S(1)} %get-tuple-element.10.refs_0_), channel_id=1, source_target_pairs={{0,32},{32,64},{64,96},{96,0},{1,33},{33,65},{65,97},{97,1},{2,34}... | collective-permute-start | bytes 491528 | tf_op jit(solution)/shard_map/ppermute | solution.py:224
  22.1 4.4 %collective-permute-start.1 = (bf16[640,128]{1,0:T(8,128)(2,1)S(1)}, bf16[640,128]{1,0:T(8,128)(2,1)S(1)}, u32[]{:S(2)}, u32[]{:S(2)}) collective-permute-start(bf16[640,128]{1,0:T(8,128)(2,1)S(1)} %get-tuple-element.10.refs_0_), channel_id=1, source_target_pairs={{0,64},{32,96},{64,0},{96,32},{1,65},{33,97},{65,1},{97,33},{2,66}... | collective-permute-start | bytes 491528 | tf_op jit(solution)/shard_map/ppermute | solution.py:224
  26.4 3.1 %collective-permute-start.2 = (bf16[640,128]{1,0:T(8,128)(2,1)S(1)}, bf16[640,128]{1,0:T(8,128)(2,1)S(1)}, u32[]{:S(2)}, u32[]{:S(2)}) collective-permute-start(bf16[640,128]{1,0:T(8,128)(2,1)S(1)} %get-tuple-element.10.refs_0_), channel_id=1, source_target_pairs={{0,96},{32,0},{64,32},{96,64},{1,97},{33,1},{65,33},{97,65},{2,98}... | collective-permute-start | bytes 491528 | tf_op jit(solution)/shard_map/ppermute | solution.py:224
  29.5 0.0 copy-done
  29.5 0.8 shard_map.78
  30.3 1.6 %all-to-all-done = bf16[16,80,128]{2,1,0:T(8,128)(2,1)S(1)} async-done(((bf16[16,80,128]{2,1,0:T(8,128)(2,1)}), bf16[16,80,128]{2,1,0:T(8,128)(2,1)S(1)}, u32[]{:S(2)}, u32[]{:S(2)}) %all-to-all-start) | async-done | bytes 327712 | tf_op jit(solution)/shard_map/all_to_all | solution.py:254
  31.9 4.2 %all_gather.3.mod_ref.lat_ref = bf16[32,80,128]{2,1,0:T(8,128)(2,1)S(1)} all-gather(bf16[16,80,128]{2,1,0:T(8,128)(2,1)S(1)} %all-to-all-done), channel_id=1, replica_groups=mesh['y_lo'=4,'x'=4,'z'=8,'y_hi'=2,'core'=2] {'core'}, dimensions={0}, use_global_device_ids=true | all-gather | bytes 983040 | tf_op jit(solution)/shard_map/all_gather | solution.py:255
  36.1 0.0 collective-permute-done.refs_1_
  36.1 0.0 collective-permute-done.1.refs_2_
  36.1 0.0 collective-permute-done.2.refs_3_
  36.1 0.8 shard_map.79
  36.9 10.8 %all_to_all.20.parts_ref = bf16[4,176,128]{2,1,0:T(8,128)(2,1)S(1)} all-to-all(bf16[4,176,128]{2,1,0:T(8,128)(2,1)S(1)} %shard_map.79), channel_id=1, replica_groups=mesh['y_lo'=4,'x'=4,'z'=8,'y_hi'=2,'core'=2] {'y_lo'}, dimensions={0} | all-to-all | bytes 360448 | tf_op jit(solution)/shard_map/all_to_all | solution.py:270
  47.7 1.9 %shard_map.80 = bf16[16,32,128]{2,1,0:T(8,128)(2,1)S(1)} custom-call(bf16[4,176,128]{2,1,0:T(8,128)(2,1)S(1)} %all_to_all.20.parts_ref, bf16[32,80,128]{2,1,0:T(8,128)(2,1)S(1)} %all_gather.3.mod_ref.lat_ref, bf16[2,128,128]{2,1,0:T(8,128)(2,1)S(1)} %get-tuple-element.11.gram_ref), custom_call_target="tpu_custom_call" | custom-call | tf_op jit(solution)/shard_map/pallas_call | solution.py:234
  49.6 0.0 copy-start.1
  49.6 13.9 %all_to_all.21.shares_ref = bf16[16,32,128]{2,1,0:T(8,128)(2,1)S(1)} all-to-all(bf16[16,32,128]{2,1,0:T(8,128)(2,1)S(1)} %shard_map.80), channel_id=1, replica_groups=mesh['y_lo'=4,'x'=4,'z'=8,'y_hi'=2,'core'=2] {'z','core'}, dimensions={0} | all-to-all | bytes 262144 | tf_op jit(solution)/shard_map/all_to_all | solution.py:272
  63.6 0.0 copy-done.1
  63.6 0.7 shard_map.81
  64.3 17.0 %all_to_all.22.terms_ref = bf16[32,16,128]{2,1,0:T(8,128)(2,1)S(1)} all-to-all(bf16[32,16,128]{2,1,0:T(8,128)(2,1)S(1)} %get-tuple-element.12), channel_id=1, replica_groups=mesh['y_lo'=4,'x'=4,'z'=8,'y_hi'=2,'core'=2] {'y_lo','x','y_hi'}, dimensions={0} | all-to-all | bytes 262144 | tf_op jit(solution)/shard_map/all_to_all | solution.py:280
  81.3 1.4 %shard_map.82 = (f32[1,32,64]{2,1,0:T(8,128)}, f32[1,32,64]{2,1,0:T(8,128)}) custom-call(s32[17]{0:T(128)} %stamps_ref.5, bf16[32,16,128]{2,1,0:T(8,128)(2,1)S(1)} %all_to_all.22.terms_ref, f32[16,128]{1,0:T(8,128)S(1)} %get-tuple-element.13.own_ref, f32[1,32,64]{2,1,0:T(8,128)S(1)} %copy-done.1), custom_call_target="tpu_custom_call" | custom-call | tf_op jit(solution)/shard_map/pallas_call | solution.py:234
Async XLA Ops:
  0.6 28.9 %copy-start = (bf16[64,4096]{1,0:T(8,128)(2,1)S(1)}, bf16[64,4096]{1,0:T(8,128)(2,1)}, u32[]{:S(2)}) copy-start(bf16[64,4096]{1,0:T(8,128)(2,1)} %embed_ref.1) | copy-start | bytes 1572868
  2.7 29.2 %all-to-all-start = ((bf16[16,80,128]{2,1,0:T(8,128)(2,1)}), bf16[16,80,128]{2,1,0:T(8,128)(2,1)S(1)}, u32[]{:S(2)}, u32[]{:S(2)}) async-start(bf16[16,80,128]{2,1,0:T(8,128)(2,1)} %get-tuple-element.8), calls=%async_computation | async-start | bytes 655360 | tf_op jit(solution)/shard_map/all_to_all | solution.py:254
  18.9 17.2 %collective-permute-start = (bf16[640,128]{1,0:T(8,128)(2,1)S(1)}, bf16[640,128]{1,0:T(8,128)(2,1)S(1)}, u32[]{:S(2)}, u32[]{:S(2)}) collective-permute-start(bf16[640,128]{1,0:T(8,128)(2,1)S(1)} %get-tuple-element.10.refs_0_), channel_id=1, source_target_pairs={{0,32},{32,64},{64,96},{96,0},{1,33},{33,65},{65,97},{97,1},{2,34}... | collective-permute-start | bytes 491528 | tf_op jit(solution)/shard_map/ppermute | solution.py:224
  22.1 14.0 %collective-permute-start.1 = (bf16[640,128]{1,0:T(8,128)(2,1)S(1)}, bf16[640,128]{1,0:T(8,128)(2,1)S(1)}, u32[]{:S(2)}, u32[]{:S(2)}) collective-permute-start(bf16[640,128]{1,0:T(8,128)(2,1)S(1)} %get-tuple-element.10.refs_0_), channel_id=1, source_target_pairs={{0,64},{32,96},{64,0},{96,32},{1,65},{33,97},{65,1},{97,33},{2,66}... | collective-permute-start | bytes 491528 | tf_op jit(solution)/shard_map/ppermute | solution.py:224
  26.4 9.7 %collective-permute-start.2 = (bf16[640,128]{1,0:T(8,128)(2,1)S(1)}, bf16[640,128]{1,0:T(8,128)(2,1)S(1)}, u32[]{:S(2)}, u32[]{:S(2)}) collective-permute-start(bf16[640,128]{1,0:T(8,128)(2,1)S(1)} %get-tuple-element.10.refs_0_), channel_id=1, source_target_pairs={{0,96},{32,0},{64,32},{96,64},{1,97},{33,1},{65,33},{97,65},{2,98}... | collective-permute-start | bytes 491528 | tf_op jit(solution)/shard_map/ppermute | solution.py:224
  49.6 13.9 %copy-start.1 = (f32[1,32,64]{2,1,0:T(8,128)S(1)}, f32[1,32,64]{2,1,0:T(8,128)}, u32[]{:S(2)}) copy-start(f32[1,32,64]{2,1,0:T(8,128)} %lat_ref.5) | copy-start | bytes 24580

commit v4 on v3

--- a/solution.py
+++ b/solution.py
@@ -105,37 +105,34 @@
     total = jnp.sum(mod_ref[:, 16:80, :].astype(F32), axis=0)
     for part in range(8):
         modulation_ref[:, part * LN : (part + 1) * LN] = total[part * 8 : part * 8 + 8]
-    mq = mk = mv = 0.0
-    biases = [0.0, 0.0, 0.0]
+    m_qk = m_v = 0.0
     for far, w_ref in enumerate(w_refs):
         origin = lax.rem(place("x") + 4 - far, 4)
         own = pl.ds(pl.multiple_of(origin * 256, 256), 256)
         modulation = modulation_ref[:, own]
-        shift, scale = modulation[:4], modulation[4:] + 1.0
+        shift, scale = modulation[:4], modulation[4:]
         centered = centered_ref[:, own]
-        rows = jnp.concatenate(
-            [(centered * scale[k : k + 1]).astype(BF) for k in range(4)], axis=0
-        )
-        shift2 = jnp.concatenate(halves(shift), axis=0)
-        wq, wk = w_ref[0:256], w_ref[256:512]
-        wv = twin(w_ref[512:640].astype(F32)).astype(BF)
-        mq = mq + dot(rows, wq)
-        mk = mk + dot(rows, wk)
-        mv = mv + dot(rows, wv)
-        for j, w in enumerate((wq, wk, wv)):
-            b = dot(shift2, w)
-            biases[j] = biases[j] + b[:4] + b[4:]
+        scaled = [(centered * scale[k : k + 1]).astype(BF) for k in range(4)]
+        shifts = jnp.concatenate([*halves(shift), jnp.zeros((8, 256), BF)], axis=0)
+        rows = jnp.concatenate([*halves(centered), *scaled, shifts], axis=0)
+        m_qk = m_qk + dot(rows, jnp.concatenate([w_ref[0:256], w_ref[256:512]], axis=1))
+        m_v = m_v + dot(rows, twin(w_ref[512:640].astype(F32)).astype(BF))
     line = lax.broadcasted_iota(jnp.int32, (16, LN), 0)
     low = low_lanes((32, LN))
+    plain_qk = m_qk[0:64] + m_qk[64:128]
+    plain_v = m_v[0:64] + m_v[64:128]
     for k in range(4):
-        at = slice(k * 64, k * 64 + 64)
-        out_ref[k, 0:64] = mq[at].astype(BF)
-        out_ref[k, 64:128] = mk[at].astype(BF)
-        v = mv[at]
+        at = slice(128 + k * 64, 192 + k * 64)
+        qk = plain_qk + m_qk[at]
+        v = plain_v + m_v[at]
+        out_ref[k, 0:64] = qk[:, :LN].astype(BF)
+        out_ref[k, 64:128] = qk[:, LN:].astype(BF)
         out_ref[k, 128:160] = jnp.where(low, v[:32], v[32:]).astype(BF)
-        tile = jnp.where(line == 0, biases[0][k : k + 1], 0.0)
-        tile = jnp.where(line == 1, biases[1][k : k + 1], tile)
-        tile = jnp.where(line == 2, biases[2][k : k + 1], tile)
+        hi, lo = slice(384 + k, 385 + k), slice(388 + k, 389 + k)
+        b_qk, b_v = m_qk[hi] + m_qk[lo], m_v[hi] + m_v[lo]
+        tile = jnp.where(line == 0, b_qk[:, :LN], 0.0)
+        tile = jnp.where(line == 1, b_qk[:, LN:], tile)
+        tile = jnp.where(line == 2, b_v, tile)
         out_ref[k, 160:176] = tile.astype(BF)
 
 
@@ -146,26 +143,31 @@
     bias_q, bias_k, bias_v = total[160:161], total[161:162], total[162:163]
     packed = lat_ref[:, 0:16, :].reshape(512, LN)
     as_float = packed.astype(F32)
-    square = (dot(packed, gram_ref[0]) + dot(packed, gram_ref[1])) * as_float
+    twice = jnp.concatenate([packed, packed], axis=1)
+    square = dot(twice, gram_ref[...].reshape(256, LN)) * as_float
     low = low_lanes((512, LN))
     gain_low = lax.rsqrt(jnp.sum(jnp.where(low, square, 0.0), axis=1, keepdims=True) + 1e-06)
     gain_high = lax.rsqrt(jnp.sum(jnp.where(low, 0.0, square), axis=1, keepdims=True) + 1e-06)
-    twice = jnp.concatenate([packed, packed], axis=1)
+    none = jnp.zeros((64, 2 * LN), BF)
+    hi, lo = halves(jnp.concatenate([mq, mk], axis=1))
+    qk_low = gain_low * dot(twice, jnp.concatenate([hi, none, lo, none], axis=0))
+    qk_high = gain_high * dot(twice, jnp.concatenate([none, hi, none, lo], axis=0))
+    hi, lo = halves(mv)
     none = jnp.zeros((64, LN), BF)
-
-    def project(m, bias):
-        hi, lo = halves(m)
-        first = dot(twice, jnp.concatenate([hi, none, lo, none], axis=0))
-        second = dot(twice, jnp.concatenate([none, hi, none, lo], axis=0))
-        return gain_low * first + bias, gain_high * second + bias
+    for_low = jnp.concatenate([hi, none, lo, none], axis=0)
+    for_high = jnp.concatenate([none, hi, none, lo], axis=0)
+    v_both = dot(twice, jnp.concatenate([for_low, for_high], axis=1))
 
     def unit(u, factor):
         mean = jnp.mean(u * u, axis=1, keepdims=True)
         return (u * (lax.rsqrt(mean + 1e-06) * factor)).astype(BF)
 
-    q_low, q_high = (unit(u, math.log2(math.e) / math.sqrt(128)) for u in project(mq, bias_q))
-    keys = jnp.concatenate([unit(u, 1.0) for u in project(mk, bias_k)], axis=0)
-    values = jnp.concatenate(project(mv, bias_v), axis=0)
+    factor = math.log2(math.e) / math.sqrt(128)
+    q_low, q_high = (unit(u[:, :LN] + bias_q, factor) for u in (qk_low, qk_high))
+    keys = jnp.concatenate([unit(u[:, LN:] + bias_k, 1.0) for u in (qk_low, qk_high)], axis=0)
+    values = (
+        jnp.concatenate([gain_low * v_both[:, :LN], gain_high * v_both[:, LN:]], axis=0) + bias_v
+    )
     all_low = low_lanes((1024, LN))
     values_low = jnp.where(all_low, values, 1.0).astype(BF)
     values_high = jnp.where(all_low, 1.0, values).astype(BF)

time: 83.6 us -> 83.5 us (level)
  no operation moved by 1% of the time
where the time goes in v4:
time: 83.5 us; the launch traced here: 82.7 us
  blocking collectives  45.9 us (55%)
  starting transfers between devices  26.8 us (32%)
  Pallas kernels  7.65 us (9%)
  waiting for transfers between devices  1.65 us (2%)
    all_to_all x1, blocking collectives, stages(): terms = near(lax.all_to_all(terms, ('y_lo', 'x', 'y_hi'), 0, 0, tiled=True))  17 us
    all_to_all x1, starting transfers between devices, stages(): payload = lax.all_to_all(payload, ('z', 'y_hi'), 0, 0, tiled=True)  16.2 us
    all_to_all x1, blocking collectives, stages(): shares = near(lax.all_to_all(shares, ('z', 'core'), 0, 0, tiled=True))  13.9 us
    all_to_all x1, blocking collectives, stages(): parts = near(lax.all_to_all(parts, 'y_lo', 0, 0, tiled=True))  10.8 us
    ppermute x3, starting transfers between devices, over_x(): return lax.ppermute(w, 'x', [(i, (i + far) % 4) for i in range(4)])  10.5 us
    pallas_call x6, Pallas kernels, call(): pl.pallas_call(kernel, in_specs=[smem] * len(scalars) + [vmem] * len(args...  7.65 us
    all_gather x1, blocking collectives, stages(): gathered = near(lax.all_gather(payload, 'core', tiled=True))  4.16 us
  transfers between devices with their start and end apart: 4, of which 1 were waited for; matrix products, arithmetic and copies ran while one was open for 0% of the time, Pallas kernels for 1%

profile of v4, /device:TPU:1, one launch (start us, length us, event | category | flops | bytes accessed | tf_op | source)
XLA Modules:
  0.0 82.7 jit_solution(3064959250863401889)
XLA Ops:
  0.6 0.0 copy-start
  0.6 2.1 %shard_map.77 = (bf16[16,80,128]{2,1,0:T(8,128)(2,1)}, bf16[640,128]{1,0:T(8,128)(2,1)S(1)}) custom-call(s32[17]{0:T(128)} %stamps_ref.5, f32[1,32,64]{2,1,0:T(8,128)} %lat_ref.5, f32[8,2,4096]{2,1,0:T(2,128)} %mw_ref.1, bf16[3,256,128]{2,1,0:T(8,128)(2,1)} %bitcast.4, bf16[1,64,128]{2,1,0:T(8,128)(2,1)} %bitcast.5), custom_call_target="tpu_custom_call" | custom-call | tf_op jit(solution)/shard_map/pallas_call | solution.py:236
  2.7 16.2 %all-to-all-start = ((bf16[16,80,128]{2,1,0:T(8,128)(2,1)}), bf16[16,80,128]{2,1,0:T(8,128)(2,1)S(1)}, u32[]{:S(2)}, u32[]{:S(2)}) async-start(bf16[16,80,128]{2,1,0:T(8,128)(2,1)} %get-tuple-element.8), calls=%async_computation | async-start | bytes 655360 | tf_op jit(solution)/shard_map/all_to_all | solution.py:256
  18.9 3.1 %collective-permute-start = (bf16[640,128]{1,0:T(8,128)(2,1)S(1)}, bf16[640,128]{1,0:T(8,128)(2,1)S(1)}, u32[]{:S(2)}, u32[]{:S(2)}) collective-permute-start(bf16[640,128]{1,0:T(8,128)(2,1)S(1)} %get-tuple-element.10.refs_0_), channel_id=1, source_target_pairs={{0,32},{32,64},{64,96},{96,0},{1,33},{33,65},{65,97},{97,1},{2,34}... | collective-permute-start | bytes 491528 | tf_op jit(solution)/shard_map/ppermute | solution.py:226
  22.1 4.4 %collective-permute-start.1 = (bf16[640,128]{1,0:T(8,128)(2,1)S(1)}, bf16[640,128]{1,0:T(8,128)(2,1)S(1)}, u32[]{:S(2)}, u32[]{:S(2)}) collective-permute-start(bf16[640,128]{1,0:T(8,128)(2,1)S(1)} %get-tuple-element.10.refs_0_), channel_id=1, source_target_pairs={{0,64},{32,96},{64,0},{96,32},{1,65},{33,97},{65,1},{97,33},{2,66}... | collective-permute-start | bytes 491528 | tf_op jit(solution)/shard_map/ppermute | solution.py:226
  26.4 3.1 %collective-permute-start.2 = (bf16[640,128]{1,0:T(8,128)(2,1)S(1)}, bf16[640,128]{1,0:T(8,128)(2,1)S(1)}, u32[]{:S(2)}, u32[]{:S(2)}) collective-permute-start(bf16[640,128]{1,0:T(8,128)(2,1)S(1)} %get-tuple-element.10.refs_0_), channel_id=1, source_target_pairs={{0,96},{32,0},{64,32},{96,64},{1,97},{33,1},{65,33},{97,65},{2,98}... | collective-permute-start | bytes 491528 | tf_op jit(solution)/shard_map/ppermute | solution.py:226
  29.5 0.0 copy-done
  29.5 0.8 shard_map.78
  30.3 1.6 %all-to-all-done = bf16[16,80,128]{2,1,0:T(8,128)(2,1)S(1)} async-done(((bf16[16,80,128]{2,1,0:T(8,128)(2,1)}), bf16[16,80,128]{2,1,0:T(8,128)(2,1)S(1)}, u32[]{:S(2)}, u32[]{:S(2)}) %all-to-all-start) | async-done | bytes 327712 | tf_op jit(solution)/shard_map/all_to_all | solution.py:256
  31.9 4.2 %all_gather.3.mod_ref.lat_ref = bf16[32,80,128]{2,1,0:T(8,128)(2,1)S(1)} all-gather(bf16[16,80,128]{2,1,0:T(8,128)(2,1)S(1)} %all-to-all-done), channel_id=1, replica_groups=mesh['y_lo'=4,'x'=4,'z'=8,'y_hi'=2,'core'=2] {'core'}, dimensions={0}, use_global_device_ids=true | all-gather | bytes 983040 | tf_op jit(solution)/shard_map/all_gather | solution.py:257
  36.1 0.0 collective-permute-done.refs_1_
  36.1 0.0 collective-permute-done.1.refs_2_
  36.1 0.0 collective-permute-done.2.refs_3_
  36.1 0.7 shard_map.79
  36.8 10.8 %all_to_all.20.parts_ref = bf16[4,176,128]{2,1,0:T(8,128)(2,1)S(1)} all-to-all(bf16[4,176,128]{2,1,0:T(8,128)(2,1)S(1)} %shard_map.79), channel_id=1, replica_groups=mesh['y_lo'=4,'x'=4,'z'=8,'y_hi'=2,'core'=2] {'y_lo'}, dimensions={0} | all-to-all | bytes 360448 | tf_op jit(solution)/shard_map/all_to_all | solution.py:272
  47.7 1.9 %shard_map.80 = bf16[16,32,128]{2,1,0:T(8,128)(2,1)S(1)} custom-call(bf16[4,176,128]{2,1,0:T(8,128)(2,1)S(1)} %all_to_all.20.parts_ref, bf16[32,80,128]{2,1,0:T(8,128)(2,1)S(1)} %all_gather.3.mod_ref.lat_ref, bf16[2,128,128]{2,1,0:T(8,128)(2,1)S(1)} %get-tuple-element.11.gram_ref), custom_call_target="tpu_custom_call" | custom-call | tf_op jit(solution)/shard_map/pallas_call | solution.py:236
  49.6 0.0 copy-start.1
  49.6 13.9 %all_to_all.21.shares_ref = bf16[16,32,128]{2,1,0:T(8,128)(2,1)S(1)} all-to-all(bf16[16,32,128]{2,1,0:T(8,128)(2,1)S(1)} %shard_map.80), channel_id=1, replica_groups=mesh['y_lo'=4,'x'=4,'z'=8,'y_hi'=2,'core'=2] {'z','core'}, dimensions={0} | all-to-all | bytes 262144 | tf_op jit(solution)/shard_map/all_to_all | solution.py:274
  63.5 0.0 copy-done.1
  63.5 0.7 shard_map.81
  64.3 17.0 %all_to_all.22.terms_ref = bf16[32,16,128]{2,1,0:T(8,128)(2,1)S(1)} all-to-all(bf16[32,16,128]{2,1,0:T(8,128)(2,1)S(1)} %get-tuple-element.12), channel_id=1, replica_groups=mesh['y_lo'=4,'x'=4,'z'=8,'y_hi'=2,'core'=2] {'y_lo','x','y_hi'}, dimensions={0} | all-to-all | bytes 262144 | tf_op jit(solution)/shard_map/all_to_all | solution.py:282
  81.2 1.4 %shard_map.82 = (f32[1,32,64]{2,1,0:T(8,128)}, f32[1,32,64]{2,1,0:T(8,128)}) custom-call(s32[17]{0:T(128)} %stamps_ref.5, bf16[32,16,128]{2,1,0:T(8,128)(2,1)S(1)} %all_to_all.22.terms_ref, f32[16,128]{1,0:T(8,128)S(1)} %get-tuple-element.13.own_ref, f32[1,32,64]{2,1,0:T(8,128)S(1)} %copy-done.1), custom_call_target="tpu_custom_call" | custom-call | tf_op jit(solution)/shard_map/pallas_call | solution.py:236
Async XLA Ops:
  0.6 28.9 %copy-start = (bf16[64,4096]{1,0:T(8,128)(2,1)S(1)}, bf16[64,4096]{1,0:T(8,128)(2,1)}, u32[]{:S(2)}) copy-start(bf16[64,4096]{1,0:T(8,128)(2,1)} %embed_ref.1) | copy-start | bytes 1572868
  2.7 29.2 %all-to-all-start = ((bf16[16,80,128]{2,1,0:T(8,128)(2,1)}), bf16[16,80,128]{2,1,0:T(8,128)(2,1)S(1)}, u32[]{:S(2)}, u32[]{:S(2)}) async-start(bf16[16,80,128]{2,1,0:T(8,128)(2,1)} %get-tuple-element.8), calls=%async_computation | async-start | bytes 655360 | tf_op jit(solution)/shard_map/all_to_all | solution.py:256
  18.9 17.2 %collective-permute-start = (bf16[640,128]{1,0:T(8,128)(2,1)S(1)}, bf16[640,128]{1,0:T(8,128)(2,1)S(1)}, u32[]{:S(2)}, u32[]{:S(2)}) collective-permute-start(bf16[640,128]{1,0:T(8,128)(2,1)S(1)} %get-tuple-element.10.refs_0_), channel_id=1, source_target_pairs={{0,32},{32,64},{64,96},{96,0},{1,33},{33,65},{65,97},{97,1},{2,34}... | collective-permute-start | bytes 491528 | tf_op jit(solution)/shard_map/ppermute | solution.py:226
  22.1 14.0 %collective-permute-start.1 = (bf16[640,128]{1,0:T(8,128)(2,1)S(1)}, bf16[640,128]{1,0:T(8,128)(2,1)S(1)}, u32[]{:S(2)}, u32[]{:S(2)}) collective-permute-start(bf16[640,128]{1,0:T(8,128)(2,1)S(1)} %get-tuple-element.10.refs_0_), channel_id=1, source_target_pairs={{0,64},{32,96},{64,0},{96,32},{1,65},{33,97},{65,1},{97,33},{2,66}... | collective-permute-start | bytes 491528 | tf_op jit(solution)/shard_map/ppermute | solution.py:226
  26.4 9.7 %collective-permute-start.2 = (bf16[640,128]{1,0:T(8,128)(2,1)S(1)}, bf16[640,128]{1,0:T(8,128)(2,1)S(1)}, u32[]{:S(2)}, u32[]{:S(2)}) collective-permute-start(bf16[640,128]{1,0:T(8,128)(2,1)S(1)} %get-tuple-element.10.refs_0_), channel_id=1, source_target_pairs={{0,96},{32,0},{64,32},{96,64},{1,97},{33,1},{65,33},{97,65},{2,98}... | collective-permute-start | bytes 491528 | tf_op jit(solution)/shard_map/ppermute | solution.py:226
  49.6 13.9 %copy-start.1 = (f32[1,32,64]{2,1,0:T(8,128)S(1)}, f32[1,32,64]{2,1,0:T(8,128)}, u32[]{:S(2)}) copy-start(f32[1,32,64]{2,1,0:T(8,128)} %lat_ref.5) | copy-start | bytes 24580

commit v5 on v4

--- a/solution.py
+++ b/solution.py
@@ -85,7 +85,7 @@
         out_ref[peer] = payload
 
 
-def weights_kernel(embed_ref, centered_ref, gram_ref):
+def weights_kernel(embed_ref, _, centered_ref, gram_ref):
     embed = embed_ref[...].astype(F32)
     mean = jnp.mean(embed, axis=1, keepdims=True)
     centered_ref[...] = embed_ref[:, own_columns()].astype(F32) - mean
@@ -130,9 +130,11 @@
         out_ref[k, 128:160] = jnp.where(low, v[:32], v[32:]).astype(BF)
         hi, lo = slice(384 + k, 385 + k), slice(388 + k, 389 + k)
         b_qk, b_v = m_qk[hi] + m_qk[lo], m_v[hi] + m_v[lo]
-        tile = jnp.where(line == 0, b_qk[:, :LN], 0.0)
-        tile = jnp.where(line == 1, b_qk[:, LN:], tile)
-        tile = jnp.where(line == 2, b_v, tile)
+        tile = jnp.zeros((16, LN), F32)
+        for i, bias in enumerate((b_qk[:, :LN], b_qk[:, LN:], b_v)):
+            rounded = bias.astype(BF).astype(F32)
+            tile = jnp.where(line == i, rounded, tile)
+            tile = jnp.where(line == i + 3, bias - rounded, tile)
         out_ref[k, 160:176] = tile.astype(BF)
 
 
@@ -140,7 +142,7 @@
     total = jnp.sum(parts_ref[...].astype(F32), axis=0)
     mq, mk, mv = total[0:64], total[64:128], total[128:160]
     mv = twin(mv)
-    bias_q, bias_k, bias_v = total[160:161], total[161:162], total[162:163]
+    bias_q, bias_k, bias_v = (total[i : i + 1] + total[i + 3 : i + 4] for i in (160, 161, 162))
     packed = lat_ref[:, 0:16, :].reshape(512, LN)
     as_float = packed.astype(F32)
     twice = jnp.concatenate([packed, packed], axis=1)
@@ -258,7 +260,7 @@
     ws = {2: over_x(w, 2)}
     ws.update({far: over_x(w, far) for far in (1, 3)})
     centered, gram = call(
-        weights_kernel, [vmem((64, 1024), F32), vmem((2, LN, LN), BF)], near(embed_weight)
+        weights_kernel, [vmem((64, 1024), F32), vmem((2, LN, LN), BF)], near(embed_weight), gathered
     )
     (parts,) = call(
         partial_kernel,

time: 83.5 us -> 83.6 us (level)
  waiting for transfers between devices: 1.65 us -> 3.53 us
  starting transfers between devices: 26.8 us -> 25.7 us
    all_to_all x1, waiting for transfers between devices: 1.64 us -> 3.52 us  [stages(): payload = lax.all_to_all(payload, ('z', 'y_hi'), 0, 0, tiled=True)]
    ppermute x3, starting transfers between devices: 10.5 us -> 9.46 us  [over_x(): return lax.ppermute(w, 'x', [(i, (i + far) % 4) for i in range(4)])]
    all_to_all x1, blocking collectives: 17 us -> 16 us  [stages(): terms = near(lax.all_to_all(terms, ('y_lo', 'x', 'y_hi'), 0, 0, tiled=True))]
where the time goes in v5:
time: 83.6 us; the launch traced here: 82.7 us
  blocking collectives  45.2 us (54%)
  starting transfers between devices  25.7 us (31%)
  Pallas kernels  7.59 us (9%)
  waiting for transfers between devices  3.53 us (4%)
    all_to_all x1, starting transfers between devices, stages(): payload = lax.all_to_all(payload, ('z', 'y_hi'), 0, 0, tiled=True)  16.2 us
    all_to_all x1, blocking collectives, stages(): terms = near(lax.all_to_all(terms, ('y_lo', 'x', 'y_hi'), 0, 0, tiled=True))  16 us
    all_to_all x1, blocking collectives, stages(): shares = near(lax.all_to_all(shares, ('z', 'core'), 0, 0, tiled=True))  14.2 us
    all_to_all x1, blocking collectives, stages(): parts = near(lax.all_to_all(parts, 'y_lo', 0, 0, tiled=True))  10.8 us
    ppermute x3, starting transfers between devices, over_x(): return lax.ppermute(w, 'x', [(i, (i + far) % 4) for i in range(4)])  9.46 us
    pallas_call x6, Pallas kernels, call(): pl.pallas_call(kernel, in_specs=[smem] * len(scalars) + [vmem] * len(args...  7.59 us
    all_gather x1, blocking collectives, stages(): gathered = near(lax.all_gather(payload, 'core', tiled=True))  4.15 us
    all_to_all x1, waiting for transfers between devices, stages(): payload = lax.all_to_all(payload, ('z', 'y_hi'), 0, 0, tiled=True)  3.52 us
  transfers between devices with their start and end apart: 4, of which 1 were waited for; matrix products, arithmetic and copies ran while one was open for 0% of the time, Pallas kernels for 1%

profile of v5, /device:TPU:1, one launch (start us, length us, event | category | flops | bytes accessed | tf_op | source)
XLA Modules:
  0.0 82.7 jit_solution(10292596498713256091)
XLA Ops:
  0.6 2.0 %shard_map.77 = (bf16[16,80,128]{2,1,0:T(8,128)(2,1)}, bf16[640,128]{1,0:T(8,128)(2,1)S(1)}) custom-call(s32[17]{0:T(128)} %stamps_ref.5, f32[1,32,64]{2,1,0:T(8,128)} %lat_ref.5, f32[8,2,4096]{2,1,0:T(2,128)} %mw_ref.1, bf16[3,256,128]{2,1,0:T(8,128)(2,1)} %bitcast.4, bf16[1,64,128]{2,1,0:T(8,128)(2,1)} %bitcast.5), custom_call_target="tpu_custom_call" | custom-call | tf_op jit(solution)/shard_map/pallas_call | solution.py:238
  2.6 16.2 %all-to-all-start = ((bf16[16,80,128]{2,1,0:T(8,128)(2,1)}), bf16[16,80,128]{2,1,0:T(8,128)(2,1)S(1)}, u32[]{:S(2)}, u32[]{:S(2)}) async-start(bf16[16,80,128]{2,1,0:T(8,128)(2,1)} %get-tuple-element.8), calls=%async_computation | async-start | bytes 655360 | tf_op jit(solution)/shard_map/all_to_all | solution.py:258
  18.9 0.0 copy-start
  18.9 4.5 %collective-permute-start.2 = (bf16[640,128]{1,0:T(8,128)(2,1)S(1)}, bf16[640,128]{1,0:T(8,128)(2,1)S(1)}, u32[]{:S(2)}, u32[]{:S(2)}) collective-permute-start(bf16[640,128]{1,0:T(8,128)(2,1)S(1)} %get-tuple-element.10.refs_0_), channel_id=1, source_target_pairs={{0,96},{32,0},{64,32},{96,64},{1,97},{33,1},{65,33},{97,65},{2,98}... | collective-permute-start | bytes 491528 | tf_op jit(solution)/shard_map/ppermute | solution.py:228
  23.4 2.4 %collective-permute-start.1 = (bf16[640,128]{1,0:T(8,128)(2,1)S(1)}, bf16[640,128]{1,0:T(8,128)(2,1)S(1)}, u32[]{:S(2)}, u32[]{:S(2)}) collective-permute-start(bf16[640,128]{1,0:T(8,128)(2,1)S(1)} %get-tuple-element.10.refs_0_), channel_id=1, source_target_pairs={{0,64},{32,96},{64,0},{96,32},{1,65},{33,97},{65,1},{97,33},{2,66}... | collective-permute-start | bytes 491528 | tf_op jit(solution)/shard_map/ppermute | solution.py:228
  25.8 2.5 %collective-permute-start = (bf16[640,128]{1,0:T(8,128)(2,1)S(1)}, bf16[640,128]{1,0:T(8,128)(2,1)S(1)}, u32[]{:S(2)}, u32[]{:S(2)}) collective-permute-start(bf16[640,128]{1,0:T(8,128)(2,1)S(1)} %get-tuple-element.10.refs_0_), channel_id=1, source_target_pairs={{0,32},{32,64},{64,96},{96,0},{1,33},{33,65},{65,97},{97,1},{2,34}... | collective-permute-start | bytes 491528 | tf_op jit(solution)/shard_map/ppermute | solution.py:228
  28.4 3.5 %all-to-all-done = bf16[16,80,128]{2,1,0:T(8,128)(2,1)S(1)} async-done(((bf16[16,80,128]{2,1,0:T(8,128)(2,1)}), bf16[16,80,128]{2,1,0:T(8,128)(2,1)S(1)}, u32[]{:S(2)}, u32[]{:S(2)}) %all-to-all-start) | async-done | bytes 327712 | tf_op jit(solution)/shard_map/all_to_all | solution.py:258
  31.9 4.2 %all_gather.3._.mod_ref.lat_ref = bf16[32,80,128]{2,1,0:T(8,128)(2,1)S(1)} all-gather(bf16[16,80,128]{2,1,0:T(8,128)(2,1)S(1)} %all-to-all-done), channel_id=1, replica_groups=mesh['y_lo'=4,'x'=4,'z'=8,'y_hi'=2,'core'=2] {'core'}, dimensions={0}, use_global_device_ids=true | all-gather | bytes 983040 | tf_op jit(solution)/shard_map/all_gather | solution.py:259
  36.0 0.0 copy-done
  36.0 0.8 shard_map.78
  36.8 0.0 collective-permute-done.2.refs_3_
  36.8 0.0 collective-permute-done.1.refs_2_
  36.9 0.0 collective-permute-done.refs_1_
  36.9 0.7 shard_map.79
  37.6 10.8 %all_to_all.20.parts_ref = bf16[4,176,128]{2,1,0:T(8,128)(2,1)S(1)} all-to-all(bf16[4,176,128]{2,1,0:T(8,128)(2,1)S(1)} %shard_map.79), channel_id=1, replica_groups=mesh['y_lo'=4,'x'=4,'z'=8,'y_hi'=2,'core'=2] {'y_lo'}, dimensions={0} | all-to-all | bytes 360448 | tf_op jit(solution)/shard_map/all_to_all | solution.py:274
  48.4 1.9 %shard_map.80 = bf16[16,32,128]{2,1,0:T(8,128)(2,1)S(1)} custom-call(bf16[4,176,128]{2,1,0:T(8,128)(2,1)S(1)} %all_to_all.20.parts_ref, bf16[32,80,128]{2,1,0:T(8,128)(2,1)S(1)} %all_gather.3._.mod_ref.lat_ref, bf16[2,128,128]{2,1,0:T(8,128)(2,1)S(1)} %get-tuple-element.11.gram_ref), custom_call_target="tpu_custom_call" | custom-call | tf_op jit(solution)/shard_map/pallas_call | solution.py:238
  50.3 0.0 copy-start.1
  50.3 14.2 %all_to_all.21.shares_ref = bf16[16,32,128]{2,1,0:T(8,128)(2,1)S(1)} all-to-all(bf16[16,32,128]{2,1,0:T(8,128)(2,1)S(1)} %shard_map.80), channel_id=1, replica_groups=mesh['y_lo'=4,'x'=4,'z'=8,'y_hi'=2,'core'=2] {'z','core'}, dimensions={0} | all-to-all | bytes 262144 | tf_op jit(solution)/shard_map/all_to_all | solution.py:276
  64.5 0.0 copy-done.1
  64.5 0.7 shard_map.81
  65.3 16.0 %all_to_all.22.terms_ref = bf16[32,16,128]{2,1,0:T(8,128)(2,1)S(1)} all-to-all(bf16[32,16,128]{2,1,0:T(8,128)(2,1)S(1)} %get-tuple-element.12), channel_id=1, replica_groups=mesh['y_lo'=4,'x'=4,'z'=8,'y_hi'=2,'core'=2] {'y_lo','x','y_hi'}, dimensions={0} | all-to-all | bytes 262144 | tf_op jit(solution)/shard_map/all_to_all | solution.py:284
  81.3 1.4 %shard_map.82 = (f32[1,32,64]{2,1,0:T(8,128)}, f32[1,32,64]{2,1,0:T(8,128)}) custom-call(s32[17]{0:T(128)} %stamps_ref.5, bf16[32,16,128]{2,1,0:T(8,128)(2,1)S(1)} %all_to_all.22.terms_ref, f32[16,128]{1,0:T(8,128)S(1)} %get-tuple-element.13.own_ref, f32[1,32,64]{2,1,0:T(8,128)S(1)} %copy-done.1), custom_call_target="tpu_custom_call" | custom-call | tf_op jit(solution)/shard_map/pallas_call | solution.py:238
Async XLA Ops:
  2.6 29.2 %all-to-all-start = ((bf16[16,80,128]{2,1,0:T(8,128)(2,1)}), bf16[16,80,128]{2,1,0:T(8,128)(2,1)S(1)}, u32[]{:S(2)}, u32[]{:S(2)}) async-start(bf16[16,80,128]{2,1,0:T(8,128)(2,1)} %get-tuple-element.8), calls=%async_computation | async-start | bytes 655360 | tf_op jit(solution)/shard_map/all_to_all | solution.py:258
  18.9 17.2 %copy-start = (bf16[64,4096]{1,0:T(8,128)(2,1)S(1)}, bf16[64,4096]{1,0:T(8,128)(2,1)}, u32[]{:S(2)}) copy-start(bf16[64,4096]{1,0:T(8,128)(2,1)} %embed_ref.1) | copy-start | bytes 1572868
  18.9 18.0 %collective-permute-start.2 = (bf16[640,128]{1,0:T(8,128)(2,1)S(1)}, bf16[640,128]{1,0:T(8,128)(2,1)S(1)}, u32[]{:S(2)}, u32[]{:S(2)}) collective-permute-start(bf16[640,128]{1,0:T(8,128)(2,1)S(1)} %get-tuple-element.10.refs_0_), channel_id=1, source_target_pairs={{0,96},{32,0},{64,32},{96,64},{1,97},{33,1},{65,33},{97,65},{2,98}... | collective-permute-start | bytes 491528 | tf_op jit(solution)/shard_map/ppermute | solution.py:228
  23.4 13.4 %collective-permute-start.1 = (bf16[640,128]{1,0:T(8,128)(2,1)S(1)}, bf16[640,128]{1,0:T(8,128)(2,1)S(1)}, u32[]{:S(2)}, u32[]{:S(2)}) collective-permute-start(bf16[640,128]{1,0:T(8,128)(2,1)S(1)} %get-tuple-element.10.refs_0_), channel_id=1, source_target_pairs={{0,64},{32,96},{64,0},{96,32},{1,65},{33,97},{65,1},{97,33},{2,66}... | collective-permute-start | bytes 491528 | tf_op jit(solution)/shard_map/ppermute | solution.py:228
  25.8 11.0 %collective-permute-start = (bf16[640,128]{1,0:T(8,128)(2,1)S(1)}, bf16[640,128]{1,0:T(8,128)(2,1)S(1)}, u32[]{:S(2)}, u32[]{:S(2)}) collective-permute-start(bf16[640,128]{1,0:T(8,128)(2,1)S(1)} %get-tuple-element.10.refs_0_), channel_id=1, source_target_pairs={{0,32},{32,64},{64,96},{96,0},{1,33},{33,65},{65,97},{97,1},{2,34}... | collective-permute-start | bytes 491528 | tf_op jit(solution)/shard_map/ppermute | solution.py:228
  50.3 14.2 %copy-start.1 = (f32[1,32,64]{2,1,0:T(8,128)S(1)}, f32[1,32,64]{2,1,0:T(8,128)}, u32[]{:S(2)}) copy-start(f32[1,32,64]{2,1,0:T(8,128)} %lat_ref.5) | copy-start | bytes 24580

commit v6 on v5

--- a/solution.py
+++ b/solution.py
@@ -69,7 +69,8 @@
     return jnp.concatenate([jnp.where(low, lines, turned), jnp.where(low, turned, lines)], axis=0)
 
 
-def pack_kernel(stamps_ref, lat_ref, mw_ref, w_ref, out_weight_ref, out_ref, folded_ref):
+def pack_kernel(stamps_ref, lat_ref, mw_ref, w_ref, out_weight_ref, out_ref, folded_ref, size_ref):
+    size_ref[...] = step_of(stamps_ref, place(*STEP))
     out = out_weight_ref[0]
     wv = dot_t(w_ref[2], jnp.concatenate([out, out], axis=0))
     folded_ref[0:512] = w_ref[0:2].reshape(512, LN)
@@ -194,10 +195,10 @@
     return width.astype(F32) / 1000.0
 
 
-def increments_kernel(stamps_ref, shares_ref, lat_ref, out_ref, own_ref):
+def increments_kernel(size_ref, shares_ref, lat_ref, out_ref, own_ref):
     step, side = place(*STEP), place("y_hi")
     velocity = jnp.sum(shares_ref[...].astype(F32), axis=0)
-    size = step_of(stamps_ref, step)
+    size = size_ref[...]
     start = jnp.where(step == 0, pack_rows(lat_ref[0]), 0.0)
     for part in range(2):
         mine = velocity[part * 16 : part * 16 + 16]
@@ -208,10 +209,10 @@
     own_ref[...] = jnp.where(side == 0, velocity[:16], velocity[16:])
 
 
-def finish_kernel(stamps_ref, terms_ref, own_ref, lat_ref, updated_ref, velocity_ref):
+def finish_kernel(size_ref, terms_ref, own_ref, lat_ref, updated_ref, velocity_ref):
     step, side = place(*STEP), place("y_hi")
     own = own_ref[...]
-    size = step_of(stamps_ref, step)
+    size = size_ref[...]
     other = terms_ref[step * 2 + 1 - side].astype(F32)
     start = jnp.where(step == 0, pack_rows(lat_ref[0]), 0.0)
     velocity = own + other / size
@@ -246,9 +247,9 @@
 
 def stages(latents, timesteps, embed_weight, mod_weight, qkv_weight, out_weight):
     vmem = pltpu.VMEM
-    payload, w = call(
+    payload, w, size = call(
         pack_kernel,
-        [vmem((16, 80, LN), BF), vmem((640, LN), BF)],
+        [vmem((16, 80, LN), BF), vmem((640, LN), BF), vmem((16, LN), F32)],
         latents,
         mod_weight,
         jnp.moveaxis(qkv_weight[:, 0], 1, 0),
@@ -258,7 +259,8 @@
     payload = lax.all_to_all(payload, ("z", "y_hi"), 0, 0, tiled=True)
     gathered = near(lax.all_gather(payload, "core", tiled=True))
     ws = {2: over_x(w, 2)}
-    ws.update({far: over_x(w, far) for far in (1, 3)})
+    for far in (1, 3):
+        ws[far] = over_x(w, far)
     centered, gram = call(
         weights_kernel, [vmem((64, 1024), F32), vmem((2, LN, LN), BF)], near(embed_weight), gathered
     )
@@ -277,15 +279,13 @@
     terms, own = call(
         increments_kernel,
         [vmem((32, 16, LN), BF), vmem((16, LN), F32)],
+        near(size),
         shares,
         near(latents),
-        scalars=(timesteps,),
     )
     terms = near(lax.all_to_all(terms, ("y_lo", "x", "y_hi"), 0, 0, tiled=True))
     out = jax.ShapeDtypeStruct(latents.shape, F32)
-    return tuple(
-        call(finish_kernel, [out, out], terms, near(own), near(latents), scalars=(timesteps,))
-    )
+    return tuple(call(finish_kernel, [out, out], near(size), terms, near(own), near(latents)))
 
 
 def solution(mesh):

time: 83.6 us -> 82.2 us (0.983)
  Pallas kernels: 7.59 us -> 6.28 us
    pallas_call x6, Pallas kernels: 7.59 us -> 6.28 us  [call(): pl.pallas_call(kernel, in_specs=[smem] * len(scalars) + [vmem] * len(args...]
where the time goes in v6:
time: 82.2 us; the launch traced here: 81.4 us
  blocking collectives  45.2 us (55%)
  starting transfers between devices  25.7 us (31%)
  Pallas kernels  6.28 us (8%)
  waiting for transfers between devices  3.52 us (4%)
    all_to_all x1, starting transfers between devices, stages(): payload = lax.all_to_all(payload, ('z', 'y_hi'), 0, 0, tiled=True)  16.2 us
    all_to_all x1, blocking collectives, stages(): terms = near(lax.all_to_all(terms, ('y_lo', 'x', 'y_hi'), 0, 0, tiled=True))  16 us
    all_to_all x1, blocking collectives, stages(): shares = near(lax.all_to_all(shares, ('z', 'core'), 0, 0, tiled=True))  14.2 us
    all_to_all x1, blocking collectives, stages(): parts = near(lax.all_to_all(parts, 'y_lo', 0, 0, tiled=True))  10.8 us
    ppermute x3, starting transfers between devices, over_x(): return lax.ppermute(w, 'x', [(i, (i + far) % 4) for i in range(4)])  9.46 us
    pallas_call x6, Pallas kernels, call(): pl.pallas_call(kernel, in_specs=[smem] * len(scalars) + [vmem] * len(args...  6.28 us
    all_gather x1, blocking collectives, stages(): gathered = near(lax.all_gather(payload, 'core', tiled=True))  4.16 us
    all_to_all x1, waiting for transfers between devices, stages(): payload = lax.all_to_all(payload, ('z', 'y_hi'), 0, 0, tiled=True)  3.51 us
  transfers between devices with their start and end apart: 4, of which 1 were waited for; matrix products, arithmetic and copies ran while one was open for 0% of the time, Pallas kernels for 1%

profile of v6, /device:TPU:1, one launch (start us, length us, event | category | flops | bytes accessed | tf_op | source)
XLA Modules:
  0.0 81.4 jit_solution(11643383594435584610)
XLA Ops:
  0.6 2.0 %shard_map.77 = (bf16[16,80,128]{2,1,0:T(8,128)(2,1)}, bf16[640,128]{1,0:T(8,128)(2,1)S(1)}, f32[16,128]{1,0:T(8,128)S(1)}) custom-call(s32[17]{0:T(128)} %stamps_ref.1, f32[1,32,64]{2,1,0:T(8,128)} %lat_ref.5, f32[8,2,4096]{2,1,0:T(2,128)} %mw_ref.1, bf16[3,256,128]{2,1,0:T(8,128)(2,1)} %bitcast.4, bf16[1,64,128]{2,1,0:T(8,128)(2,1)} %bitcast.5), custom_call_target="tpu_custom_call" | custom-call | tf_op jit(solution)/shard_map/pallas_call | solution.py:239
  2.6 16.2 %all-to-all-start = ((bf16[16,80,128]{2,1,0:T(8,128)(2,1)}), bf16[16,80,128]{2,1,0:T(8,128)(2,1)S(1)}, u32[]{:S(2)}, u32[]{:S(2)}) async-start(bf16[16,80,128]{2,1,0:T(8,128)(2,1)} %get-tuple-element.10), calls=%async_computation | async-start | bytes 655360 | tf_op jit(solution)/shard_map/all_to_all | solution.py:259
  18.9 0.0 copy-start
  18.9 4.5 %collective-permute-start.2 = (bf16[640,128]{1,0:T(8,128)(2,1)S(1)}, bf16[640,128]{1,0:T(8,128)(2,1)S(1)}, u32[]{:S(2)}, u32[]{:S(2)}) collective-permute-start(bf16[640,128]{1,0:T(8,128)(2,1)S(1)} %get-tuple-element.12.refs_0_), channel_id=1, source_target_pairs={{0,96},{32,0},{64,32},{96,64},{1,97},{33,1},{65,33},{97,65},{2,98}... | collective-permute-start | bytes 491528 | tf_op jit(solution)/shard_map/ppermute | solution.py:229
  23.4 2.4 %collective-permute-start.1 = (bf16[640,128]{1,0:T(8,128)(2,1)S(1)}, bf16[640,128]{1,0:T(8,128)(2,1)S(1)}, u32[]{:S(2)}, u32[]{:S(2)}) collective-permute-start(bf16[640,128]{1,0:T(8,128)(2,1)S(1)} %get-tuple-element.12.refs_0_), channel_id=1, source_target_pairs={{0,64},{32,96},{64,0},{96,32},{1,65},{33,97},{65,1},{97,33},{2,66}... | collective-permute-start | bytes 491528 | tf_op jit(solution)/shard_map/ppermute | solution.py:229
  25.9 2.5 %collective-permute-start = (bf16[640,128]{1,0:T(8,128)(2,1)S(1)}, bf16[640,128]{1,0:T(8,128)(2,1)S(1)}, u32[]{:S(2)}, u32[]{:S(2)}) collective-permute-start(bf16[640,128]{1,0:T(8,128)(2,1)S(1)} %get-tuple-element.12.refs_0_), channel_id=1, source_target_pairs={{0,32},{32,64},{64,96},{96,0},{1,33},{33,65},{65,97},{97,1},{2,34}... | collective-permute-start | bytes 491528 | tf_op jit(solution)/shard_map/ppermute | solution.py:229
  28.4 3.5 %all-to-all-done = bf16[16,80,128]{2,1,0:T(8,128)(2,1)S(1)} async-done(((bf16[16,80,128]{2,1,0:T(8,128)(2,1)}), bf16[16,80,128]{2,1,0:T(8,128)(2,1)S(1)}, u32[]{:S(2)}, u32[]{:S(2)}) %all-to-all-start) | async-done | bytes 327712 | tf_op jit(solution)/shard_map/all_to_all | solution.py:259
  31.9 4.2 %all_gather.3._.mod_ref.lat_ref = bf16[32,80,128]{2,1,0:T(8,128)(2,1)S(1)} all-gather(bf16[16,80,128]{2,1,0:T(8,128)(2,1)S(1)} %all-to-all-done), channel_id=1, replica_groups=mesh['y_lo'=4,'x'=4,'z'=8,'y_hi'=2,'core'=2] {'core'}, dimensions={0}, use_global_device_ids=true | all-gather | bytes 983040 | tf_op jit(solution)/shard_map/all_gather | solution.py:260
  36.0 0.0 copy-done
  36.0 0.8 shard_map.78
  36.8 0.0 collective-permute-done.2.refs_3_
  36.8 0.0 collective-permute-done.1.refs_2_
  36.9 0.0 collective-permute-done.refs_1_
  36.9 0.7 shard_map.79
  37.6 10.8 %all_to_all.20.parts_ref = bf16[4,176,128]{2,1,0:T(8,128)(2,1)S(1)} all-to-all(bf16[4,176,128]{2,1,0:T(8,128)(2,1)S(1)} %shard_map.79), channel_id=1, replica_groups=mesh['y_lo'=4,'x'=4,'z'=8,'y_hi'=2,'core'=2] {'y_lo'}, dimensions={0} | all-to-all | bytes 360448 | tf_op jit(solution)/shard_map/all_to_all | solution.py:276
  48.4 1.9 %shard_map.80 = bf16[16,32,128]{2,1,0:T(8,128)(2,1)S(1)} custom-call(bf16[4,176,128]{2,1,0:T(8,128)(2,1)S(1)} %all_to_all.20.parts_ref, bf16[32,80,128]{2,1,0:T(8,128)(2,1)S(1)} %all_gather.3._.mod_ref.lat_ref, bf16[2,128,128]{2,1,0:T(8,128)(2,1)S(1)} %get-tuple-element.13.gram_ref), custom_call_target="tpu_custom_call" | custom-call | tf_op jit(solution)/shard_map/pallas_call | solution.py:239
  50.3 0.0 copy-start.1
  50.3 14.2 %all_to_all.21.shares_ref = bf16[16,32,128]{2,1,0:T(8,128)(2,1)S(1)} all-to-all(bf16[16,32,128]{2,1,0:T(8,128)(2,1)S(1)} %shard_map.80), channel_id=1, replica_groups=mesh['y_lo'=4,'x'=4,'z'=8,'y_hi'=2,'core'=2] {'z','core'}, dimensions={0} | all-to-all | bytes 262144 | tf_op jit(solution)/shard_map/all_to_all | solution.py:278
  64.5 0.0 copy-done.1
  64.5 0.1 shard_map.81
  64.6 16.0 %all_to_all.22.terms_ref = bf16[32,16,128]{2,1,0:T(8,128)(2,1)S(1)} all-to-all(bf16[32,16,128]{2,1,0:T(8,128)(2,1)S(1)} %get-tuple-element.14), channel_id=1, replica_groups=mesh['y_lo'=4,'x'=4,'z'=8,'y_hi'=2,'core'=2] {'y_lo','x','y_hi'}, dimensions={0} | all-to-all | bytes 262144 | tf_op jit(solution)/shard_map/all_to_all | solution.py:286
  80.6 0.8 shard_map.82
Async XLA Ops:
  2.6 29.2 %all-to-all-start = ((bf16[16,80,128]{2,1,0:T(8,128)(2,1)}), bf16[16,80,128]{2,1,0:T(8,128)(2,1)S(1)}, u32[]{:S(2)}, u32[]{:S(2)}) async-start(bf16[16,80,128]{2,1,0:T(8,128)(2,1)} %get-tuple-element.10), calls=%async_computation | async-start | bytes 655360 | tf_op jit(solution)/shard_map/all_to_all | solution.py:259
  18.9 17.2 %copy-start = (bf16[64,4096]{1,0:T(8,128)(2,1)S(1)}, bf16[64,4096]{1,0:T(8,128)(2,1)}, u32[]{:S(2)}) copy-start(bf16[64,4096]{1,0:T(8,128)(2,1)} %embed_ref.1) | copy-start | bytes 1572868
  18.9 18.0 %collective-permute-start.2 = (bf16[640,128]{1,0:T(8,128)(2,1)S(1)}, bf16[640,128]{1,0:T(8,128)(2,1)S(1)}, u32[]{:S(2)}, u32[]{:S(2)}) collective-permute-start(bf16[640,128]{1,0:T(8,128)(2,1)S(1)} %get-tuple-element.12.refs_0_), channel_id=1, source_target_pairs={{0,96},{32,0},{64,32},{96,64},{1,97},{33,1},{65,33},{97,65},{2,98}... | collective-permute-start | bytes 491528 | tf_op jit(solution)/shard_map/ppermute | solution.py:229
  23.4 13.4 %collective-permute-start.1 = (bf16[640,128]{1,0:T(8,128)(2,1)S(1)}, bf16[640,128]{1,0:T(8,128)(2,1)S(1)}, u32[]{:S(2)}, u32[]{:S(2)}) collective-permute-start(bf16[640,128]{1,0:T(8,128)(2,1)S(1)} %get-tuple-element.12.refs_0_), channel_id=1, source_target_pairs={{0,64},{32,96},{64,0},{96,32},{1,65},{33,97},{65,1},{97,33},{2,66}... | collective-permute-start | bytes 491528 | tf_op jit(solution)/shard_map/ppermute | solution.py:229
  25.9 11.0 %collective-permute-start = (bf16[640,128]{1,0:T(8,128)(2,1)S(1)}, bf16[640,128]{1,0:T(8,128)(2,1)S(1)}, u32[]{:S(2)}, u32[]{:S(2)}) collective-permute-start(bf16[640,128]{1,0:T(8,128)(2,1)S(1)} %get-tuple-element.12.refs_0_), channel_id=1, source_target_pairs={{0,32},{32,64},{64,96},{96,0},{1,33},{33,65},{65,97},{97,1},{2,34}... | collective-permute-start | bytes 491528 | tf_op jit(solution)/shard_map/ppermute | solution.py:229
  50.3 14.2 %copy-start.1 = (f32[1,32,64]{2,1,0:T(8,128)S(1)}, f32[1,32,64]{2,1,0:T(8,128)}, u32[]{:S(2)}) copy-start(f32[1,32,64]{2,1,0:T(8,128)} %lat_ref.5) | copy-start | bytes 24580

commit v7 on v6

--- a/solution.py
+++ b/solution.py
@@ -48,17 +48,27 @@
     return pl.ds(pl.multiple_of(place("y_lo") * 1024, 1024), 1024)
 
 
+def stamp_at(stamps_ref, index):
+    stamps = stamps_ref[...].astype(F32)
+    col = lax.broadcasted_iota(jnp.int32, stamps.shape, 1)
+    return jnp.sum(jnp.where(col == index, stamps, 0.0), axis=1, keepdims=True)
+
+
+def step_of(stamps_ref, step):
+    return (stamp_at(stamps_ref, step + 1) - stamp_at(stamps_ref, step)) / 1000.0
+
+
 def conditions(stamps_ref):
     shape = (8, 16)
     row = lax.broadcasted_iota(jnp.int32, shape, 0)
     col = lax.broadcasted_iota(jnp.int32, shape, 1)
-    stamp = jnp.zeros(shape, jnp.int32)
+    stamp = jnp.zeros(shape, F32)
     for k in range(4):
-        stamp = jnp.where(row % 4 == k, stamps_ref[k * 4 + place("x")], stamp)
+        stamp = jnp.where(row % 4 == k, stamp_at(stamps_ref, k * 4 + place("x")), stamp)
     feature = place(*SEQ) * 8 + col % 8
     half_count = 128
     frequencies = jnp.exp(-math.log(10000.0) * (feature % half_count).astype(F32) / half_count)
-    angles = stamp.astype(F32) * frequencies
+    angles = stamp * frequencies
     value = jnp.where(feature < half_count, jnp.cos(angles), jnp.sin(angles))
     return jnp.where(row // 4 == col // 8, value, 0.0)
 
@@ -70,7 +80,7 @@
 
 
 def pack_kernel(stamps_ref, lat_ref, mw_ref, w_ref, out_weight_ref, out_ref, folded_ref, size_ref):
-    size_ref[...] = step_of(stamps_ref, place(*STEP))
+    size_ref[...] = jnp.broadcast_to(step_of(stamps_ref, place(*STEP)), size_ref.shape)
     out = out_weight_ref[0]
     wv = dot_t(w_ref[2], jnp.concatenate([out, out], axis=0))
     folded_ref[0:512] = w_ref[0:2].reshape(512, LN)
@@ -190,11 +200,6 @@
             out_ref[z * 2 + core] = shares[z * 32 : z * 32 + 32]
 
 
-def step_of(stamps_ref, step):
-    width = jnp.full((16, LN), stamps_ref[step + 1] - stamps_ref[step], jnp.int32)
-    return width.astype(F32) / 1000.0
-
-
 def increments_kernel(size_ref, shares_ref, lat_ref, out_ref, own_ref):
     step, side = place(*STEP), place("y_hi")
     velocity = jnp.sum(shares_ref[...].astype(F32), axis=0)
@@ -250,11 +255,11 @@
     payload, w, size = call(
         pack_kernel,
         [vmem((16, 80, LN), BF), vmem((640, LN), BF), vmem((16, LN), F32)],
+        timesteps[None],
         latents,
         mod_weight,
         jnp.moveaxis(qkv_weight[:, 0], 1, 0),
         jnp.swapaxes(out_weight, 1, 2),
-        scalars=(timesteps,),
     )
     payload = lax.all_to_all(payload, ("z", "y_hi"), 0, 0, tiled=True)
     gathered = near(lax.all_gather(payload, "core", tiled=True))

time: 82.2 us -> 82.3 us (level)
  no operation moved by 1% of the time
where the time goes in v7:
time: 82.3 us; the launch traced here: 81.5 us
  blocking collectives  45.2 us (55%)
  starting transfers between devices  25.7 us (31%)
  Pallas kernels  6.37 us (8%)
  waiting for transfers between devices  3.52 us (4%)
    all_to_all x1, starting transfers between devices, stages(): payload = lax.all_to_all(payload, ('z', 'y_hi'), 0, 0, tiled=True)  16.2 us
    all_to_all x1, blocking collectives, stages(): terms = near(lax.all_to_all(terms, ('y_lo', 'x', 'y_hi'), 0, 0, tiled=True))  16 us
    all_to_all x1, blocking collectives, stages(): shares = near(lax.all_to_all(shares, ('z', 'core'), 0, 0, tiled=True))  14.2 us
    all_to_all x1, blocking collectives, stages(): parts = near(lax.all_to_all(parts, 'y_lo', 0, 0, tiled=True))  10.8 us
    ppermute x3, starting transfers between devices, over_x(): return lax.ppermute(w, 'x', [(i, (i + far) % 4) for i in range(4)])  9.46 us
    pallas_call x6, Pallas kernels, call(): pl.pallas_call(kernel, in_specs=[smem] * len(scalars) + [vmem] * len(args...  6.37 us
    all_gather x1, blocking collectives, stages(): gathered = near(lax.all_gather(payload, 'core', tiled=True))  4.16 us
    all_to_all x1, waiting for transfers between devices, stages(): payload = lax.all_to_all(payload, ('z', 'y_hi'), 0, 0, tiled=True)  3.51 us
  transfers between devices with their start and end apart: 4, of which 1 were waited for; matrix products, arithmetic and copies ran while one was open for 0% of the time, Pallas kernels for 1%

profile of v7, /device:TPU:1, one launch (start us, length us, event | category | flops | bytes accessed | tf_op | source)
XLA Modules:
  0.0 81.5 jit_solution(17471397814031588841)
XLA Ops:
  0.6 2.1 %shard_map.77 = (bf16[16,80,128]{2,1,0:T(8,128)(2,1)}, bf16[640,128]{1,0:T(8,128)(2,1)S(1)}, f32[16,128]{1,0:T(8,128)S(1)}) custom-call(s32[1,17]{1,0:T(1,128)} %bitcast.7, f32[1,32,64]{2,1,0:T(8,128)} %lat_ref.5, f32[8,2,4096]{2,1,0:T(2,128)} %mw_ref.1, bf16[3,256,128]{2,1,0:T(8,128)(2,1)} %bitcast.5, bf16[1,64,128]{2,1,0:T(8,128)(2,1)} %bitcast.6), custom_call_target="tpu_custom_call" | custom-call | tf_op jit(solution)/shard_map/pallas_call | solution.py:244
  2.7 16.2 %all-to-all-start = ((bf16[16,80,128]{2,1,0:T(8,128)(2,1)}), bf16[16,80,128]{2,1,0:T(8,128)(2,1)S(1)}, u32[]{:S(2)}, u32[]{:S(2)}) async-start(bf16[16,80,128]{2,1,0:T(8,128)(2,1)} %get-tuple-element.10), calls=%async_computation | async-start | bytes 655360 | tf_op jit(solution)/shard_map/all_to_all | solution.py:264
  19.0 0.0 copy-start
  19.0 4.5 %collective-permute-start.2 = (bf16[640,128]{1,0:T(8,128)(2,1)S(1)}, bf16[640,128]{1,0:T(8,128)(2,1)S(1)}, u32[]{:S(2)}, u32[]{:S(2)}) collective-permute-start(bf16[640,128]{1,0:T(8,128)(2,1)S(1)} %get-tuple-element.12.refs_0_), channel_id=1, source_target_pairs={{0,96},{32,0},{64,32},{96,64},{1,97},{33,1},{65,33},{97,65},{2,98}... | collective-permute-start | bytes 491528 | tf_op jit(solution)/shard_map/ppermute | solution.py:234
  23.5 2.4 %collective-permute-start.1 = (bf16[640,128]{1,0:T(8,128)(2,1)S(1)}, bf16[640,128]{1,0:T(8,128)(2,1)S(1)}, u32[]{:S(2)}, u32[]{:S(2)}) collective-permute-start(bf16[640,128]{1,0:T(8,128)(2,1)S(1)} %get-tuple-element.12.refs_0_), channel_id=1, source_target_pairs={{0,64},{32,96},{64,0},{96,32},{1,65},{33,97},{65,1},{97,33},{2,66}... | collective-permute-start | bytes 491528 | tf_op jit(solution)/shard_map/ppermute | solution.py:234
  25.9 2.5 %collective-permute-start = (bf16[640,128]{1,0:T(8,128)(2,1)S(1)}, bf16[640,128]{1,0:T(8,128)(2,1)S(1)}, u32[]{:S(2)}, u32[]{:S(2)}) collective-permute-start(bf16[640,128]{1,0:T(8,128)(2,1)S(1)} %get-tuple-element.12.refs_0_), channel_id=1, source_target_pairs={{0,32},{32,64},{64,96},{96,0},{1,33},{33,65},{65,97},{97,1},{2,34}... | collective-permute-start | bytes 491528 | tf_op jit(solution)/shard_map/ppermute | solution.py:234
  28.5 3.5 %all-to-all-done = bf16[16,80,128]{2,1,0:T(8,128)(2,1)S(1)} async-done(((bf16[16,80,128]{2,1,0:T(8,128)(2,1)}), bf16[16,80,128]{2,1,0:T(8,128)(2,1)S(1)}, u32[]{:S(2)}, u32[]{:S(2)}) %all-to-all-start) | async-done | bytes 327712 | tf_op jit(solution)/shard_map/all_to_all | solution.py:264
  32.0 4.2 %all_gather.3._.mod_ref.lat_ref = bf16[32,80,128]{2,1,0:T(8,128)(2,1)S(1)} all-gather(bf16[16,80,128]{2,1,0:T(8,128)(2,1)S(1)} %all-to-all-done), channel_id=1, replica_groups=mesh['y_lo'=4,'x'=4,'z'=8,'y_hi'=2,'core'=2] {'core'}, dimensions={0}, use_global_device_ids=true | all-gather | bytes 983040 | tf_op jit(solution)/shard_map/all_gather | solution.py:265
  36.1 0.0 copy-done
  36.1 0.8 shard_map.78
  36.9 0.0 collective-permute-done.2.refs_3_
  36.9 0.0 collective-permute-done.1.refs_2_
  37.0 0.0 collective-permute-done.refs_1_
  37.0 0.7 shard_map.79
  37.7 10.8 %all_to_all.20.parts_ref = bf16[4,176,128]{2,1,0:T(8,128)(2,1)S(1)} all-to-all(bf16[4,176,128]{2,1,0:T(8,128)(2,1)S(1)} %shard_map.79), channel_id=1, replica_groups=mesh['y_lo'=4,'x'=4,'z'=8,'y_hi'=2,'core'=2] {'y_lo'}, dimensions={0} | all-to-all | bytes 360448 | tf_op jit(solution)/shard_map/all_to_all | solution.py:281
  48.5 1.9 %shard_map.80 = bf16[16,32,128]{2,1,0:T(8,128)(2,1)S(1)} custom-call(bf16[4,176,128]{2,1,0:T(8,128)(2,1)S(1)} %all_to_all.20.parts_ref, bf16[32,80,128]{2,1,0:T(8,128)(2,1)S(1)} %all_gather.3._.mod_ref.lat_ref, bf16[2,128,128]{2,1,0:T(8,128)(2,1)S(1)} %get-tuple-element.13.gram_ref), custom_call_target="tpu_custom_call" | custom-call | tf_op jit(solution)/shard_map/pallas_call | solution.py:244
  50.4 0.0 copy-start.1
  50.4 14.2 %all_to_all.21.shares_ref = bf16[16,32,128]{2,1,0:T(8,128)(2,1)S(1)} all-to-all(bf16[16,32,128]{2,1,0:T(8,128)(2,1)S(1)} %shard_map.80), channel_id=1, replica_groups=mesh['y_lo'=4,'x'=4,'z'=8,'y_hi'=2,'core'=2] {'z','core'}, dimensions={0} | all-to-all | bytes 262144 | tf_op jit(solution)/shard_map/all_to_all | solution.py:283
  64.6 0.0 copy-done.1
  64.6 0.1 shard_map.81
  64.7 16.0 %all_to_all.22.terms_ref = bf16[32,16,128]{2,1,0:T(8,128)(2,1)S(1)} all-to-all(bf16[32,16,128]{2,1,0:T(8,128)(2,1)S(1)} %get-tuple-element.14), channel_id=1, replica_groups=mesh['y_lo'=4,'x'=4,'z'=8,'y_hi'=2,'core'=2] {'y_lo','x','y_hi'}, dimensions={0} | all-to-all | bytes 262144 | tf_op jit(solution)/shard_map/all_to_all | solution.py:291
  80.7 0.8 shard_map.82
Async XLA Ops:
  2.7 29.2 %all-to-all-start = ((bf16[16,80,128]{2,1,0:T(8,128)(2,1)}), bf16[16,80,128]{2,1,0:T(8,128)(2,1)S(1)}, u32[]{:S(2)}, u32[]{:S(2)}) async-start(bf16[16,80,128]{2,1,0:T(8,128)(2,1)} %get-tuple-element.10), calls=%async_computation | async-start | bytes 655360 | tf_op jit(solution)/shard_map/all_to_all | solution.py:264
  19.0 17.2 %copy-start = (bf16[64,4096]{1,0:T(8,128)(2,1)S(1)}, bf16[64,4096]{1,0:T(8,128)(2,1)}, u32[]{:S(2)}) copy-start(bf16[64,4096]{1,0:T(8,128)(2,1)} %embed_ref.1) | copy-start | bytes 1572868
  19.0 18.0 %collective-permute-start.2 = (bf16[640,128]{1,0:T(8,128)(2,1)S(1)}, bf16[640,128]{1,0:T(8,128)(2,1)S(1)}, u32[]{:S(2)}, u32[]{:S(2)}) collective-permute-start(bf16[640,128]{1,0:T(8,128)(2,1)S(1)} %get-tuple-element.12.refs_0_), channel_id=1, source_target_pairs={{0,96},{32,0},{64,32},{96,64},{1,97},{33,1},{65,33},{97,65},{2,98}... | collective-permute-start | bytes 491528 | tf_op jit(solution)/shard_map/ppermute | solution.py:234
  23.5 13.4 %collective-permute-start.1 = (bf16[640,128]{1,0:T(8,128)(2,1)S(1)}, bf16[640,128]{1,0:T(8,128)(2,1)S(1)}, u32[]{:S(2)}, u32[]{:S(2)}) collective-permute-start(bf16[640,128]{1,0:T(8,128)(2,1)S(1)} %get-tuple-element.12.refs_0_), channel_id=1, source_target_pairs={{0,64},{32,96},{64,0},{96,32},{1,65},{33,97},{65,1},{97,33},{2,66}... | collective-permute-start | bytes 491528 | tf_op jit(solution)/shard_map/ppermute | solution.py:234
  25.9 11.0 %collective-permute-start = (bf16[640,128]{1,0:T(8,128)(2,1)S(1)}, bf16[640,128]{1,0:T(8,128)(2,1)S(1)}, u32[]{:S(2)}, u32[]{:S(2)}) collective-permute-start(bf16[640,128]{1,0:T(8,128)(2,1)S(1)} %get-tuple-element.12.refs_0_), channel_id=1, source_target_pairs={{0,32},{32,64},{64,96},{96,0},{1,33},{33,65},{65,97},{97,1},{2,34}... | collective-permute-start | bytes 491528 | tf_op jit(solution)/shard_map/ppermute | solution.py:234
  50.4 14.2 %copy-start.1 = (f32[1,32,64]{2,1,0:T(8,128)S(1)}, f32[1,32,64]{2,1,0:T(8,128)}, u32[]{:S(2)}) copy-start(f32[1,32,64]{2,1,0:T(8,128)} %lat_ref.5) | copy-start | bytes 24580
